TPU v7x, 128 devices: a whole 4x4x4 slice. The times are simulated.
128 devices in a mesh: section: 8 (over z, core), expert: 16 (over y, x).
Axes of the slice: x: 4, y: 4, z: 4, core: 2. Of those that a mesh axis runs over, the one named last changes fastest.
Arguments:
- tokens_in: bfloat16 [2, 2048, 1024], P(None, 'expert'), may hold values from -6 to 6
- ln_gain: float32 [8, 1024], P('section'), may hold values from 0.1 to 1.9
- router: bfloat16 [8, 1024, 32], P('section'), may hold values from -0.1875 to 0.1875
- dense_in: bfloat16 [8, 1024, 2048], P('section'), may hold values from -0.1875 to 0.1875
- dense_out: bfloat16 [8, 2048, 1024], P('section'), may hold values from -0.125 to 0.125
- expert_in: bfloat16 [8, 32, 1024, 2048], P('section', 'expert'), may hold values from -0.1875 to 0.1875
- expert_out: bfloat16 [8, 32, 2048, 1024], P('section', 'expert'), may hold values from -0.125 to 0.125
- routes: int32 [8, 2, 2048, 1], P('section', None, 'expert'), may hold values from 0 to 31; in each aligned block of 64 rows (0 to 63, 64 to 127, ..., all dimensions but the last counted through in order) at most 4 rows name the same one
Outputs:
- tokens_out: bfloat16 [2, 2048, 1024], P(None, 'expert', 'section')
Inputs may be any that keep to these rules, and one draw needn't show every extreme that they name: Split every row of 2048 tokens of routes into aligned blocks of 64 tokens. In no block does one id occur more than 4 times, and in every draw some id occurs exactly 4 times in some block.
All inputs are finite; a program needn't handle non-finite values.
Results may differ from a plain program's by a relative error of at most 0.019.
Values may be sent and summed in bfloat16 or wider, within the bound.
No kernel may reach another device: no remote copies, remote signals or barrier semaphores. Data moves between devices by JAX's collectives and lax.ppermute only.
A program may use at most 128 MiB of HBM per device.

v0:
```python
import jax
import jax.numpy as jnp
from jax import lax
from jax.sharding import PartitionSpec as P


def passed_along(value, axis, steps):
    count = lax.axis_size(axis)
    initial, last = (max(0, -steps), min(count, count - steps))
    return lax.ppermute(value, axis, [(source, source + steps) for source in range(initial, last)])


def picked_2(value, axis, root):
    return lax.dynamic_index_in_dim(lax.all_gather(value, axis), root, 0, keepdims=False)


def expert_mlp(token_rows, weight_in, weight_out):
    activation = jax.nn.gelu(
        jnp.dot(token_rows, weight_in, preferred_element_type=jnp.float32), approximate=True
    ).astype(jnp.bfloat16)
    return jnp.dot(activation, weight_out, preferred_element_type=jnp.float32).astype(jnp.bfloat16)


def body(tokens_in, ln_gain, router, dense_in, dense_out, expert_in, expert_out, routes):
    sections = lax.axis_size("section")
    members = lax.axis_size("expert")
    section_index = lax.axis_index("section")
    micro_count, tok_dev, model_width = tokens_in.shape
    experts_all = router.shape[2]
    late_section = section_index >= sections // 2
    norm_gain = ln_gain[0]
    router_cols = router[0]
    weight_din = dense_in[0]
    weight_dout = dense_out[0]
    first_in = expert_in[0, 0]
    first_out = expert_out[0, 0]
    second_pick = jnp.where(late_section, 1, 0).astype(jnp.int32)
    second_in = lax.dynamic_index_in_dim(expert_in[0], second_pick, 0, keepdims=False)
    second_out = lax.dynamic_index_in_dim(expert_out[0], second_pick, 0, keepdims=False)
    blocks = micro_count * tok_dev // tok_dev
    capacity = 2 * (tok_dev // experts_all) * tok_dev // tok_dev
    id_blocks = routes.reshape(blocks, tok_dev)
    labels = jnp.arange(experts_all, dtype=jnp.int32)
    places = jnp.arange(experts_all * capacity, dtype=jnp.int32)

    def experts_on(incoming):
        sources = incoming.shape[0]
        slot_count = incoming.shape[2]
        slot_zero = expert_mlp(incoming[:, 0].reshape(-1, model_width), first_in, first_out)
        slot_one = expert_mlp(incoming[:, 1].reshape(-1, model_width), second_in, second_out)
        return jnp.stack(
            (
                slot_zero.reshape(sources, slot_count, model_width),
                slot_one.reshape(sources, slot_count, model_width),
            ),
            axis=1,
        )

    def dense_on(normed):
        hidden = jax.nn.gelu(
            jnp.dot(normed, weight_din, preferred_element_type=jnp.float32), approximate=True
        ).astype(jnp.bfloat16)
        return jnp.dot(hidden, weight_dout, preferred_element_type=jnp.float32)

    def empty_rows(incoming):
        return jnp.zeros(incoming.shape, jnp.bfloat16)

    def empty_dense(normed):
        return jnp.zeros((normed.shape[0], model_width), jnp.float32)

    def step(step_number, carried):
        received, collected = carried
        block_index = step_number - section_index
        active = (block_index >= 0) & (block_index < blocks)
        clipped = jnp.clip(block_index, 0, blocks - 1)
        stream = jnp.where(
            section_index == 0,
            lax.dynamic_index_in_dim(tokens_in, clipped, 0, keepdims=False),
            received,
        )
        expert_ids = lax.dynamic_index_in_dim(id_blocks, clipped, 0, keepdims=False)
        stream_float = stream.astype(jnp.float32)
        row_mean = jnp.mean(stream_float, axis=-1, keepdims=True)
        centred = stream_float - row_mean
        row_var = jnp.mean(centred * centred, axis=-1, keepdims=True)
        normed = (centred * lax.rsqrt(row_var + 1e-05) * norm_gain).astype(jnp.bfloat16)
        picked = expert_ids[:, None] == labels[None, :]
        picked_ones = picked.astype(jnp.int32)
        position = jnp.sum((jnp.cumsum(picked_ones, axis=0) - picked_ones) * picked_ones, axis=1)
        slot_index = expert_ids * capacity + position
        dispatch_table = (places[:, None] == slot_index[None, :]).astype(jnp.bfloat16)
        outgoing = jnp.dot(dispatch_table, normed, preferred_element_type=jnp.float32).astype(
            jnp.bfloat16
        )
        outgoing = outgoing.reshape(members, 2, capacity, model_width)
        expert_rows = lax.cond(
            active,
            experts_on,
            empty_rows,
            lax.all_to_all(outgoing, "expert", split_axis=0, concat_axis=0, tiled=True),
        )
        returned = lax.all_to_all(expert_rows, "expert", split_axis=0, concat_axis=0, tiled=True)
        dense_part = lax.cond(active, dense_on, empty_dense, normed)
        logits = jnp.dot(normed, router_cols, preferred_element_type=jnp.float32)
        gate_value = jax.nn.sigmoid(jnp.sum(jnp.where(picked, logits, 0.0), axis=1))
        routed = returned.reshape(-1, model_width)[slot_index].astype(jnp.float32)
        stream_new = (stream_float + dense_part + gate_value[:, None] * routed).astype(jnp.bfloat16)
        store_now = active & (section_index == sections - 1)
        collected = jnp.where(
            store_now, lax.dynamic_update_index_in_dim(collected, stream_new, clipped, 0), collected
        )
        received = passed_along(stream_new, "section", 1)
        return (received, collected)

    start_state = (
        jnp.zeros((tok_dev, model_width), jnp.bfloat16),
        jnp.zeros((blocks, tok_dev, model_width), jnp.bfloat16),
    )
    final_state = lax.fori_loop(0, sections + blocks - 1, step, start_state)
    gathered_out = picked_2(final_state[1], "section", sections - 1)
    share = model_width // sections
    return lax.dynamic_slice_in_dim(gathered_out, section_index * share, share, 2)


def solution(mesh):
    placed = (
        P(None, "expert", None),
        P("section", None),
        P("section", None, None),
        P("section", None, None),
        P("section", None, None),
        P("section", "expert", None, None),
        P("section", "expert", None, None),
        P("section", None, "expert", None),
    )
    return jax.shard_map(
        body, mesh=mesh, in_specs=placed, out_specs=P(None, "expert", "section"), check_vma=False
    )
```

profile of v0, /device:TPU:1, one launch (start us, length us, event | category | flops | bytes accessed | tf_op | source)
XLA Modules:
  0.0 478.5 jit_solution(10913487962287378654)
XLA Ops:
  6.5 8.5 %dynamic-slice_bitcast_fusion.1 = (bf16[1024,2048]{1,0:T(8,128)(2,1)}, bf16[1024,2048]{1,0:T(8,128)(2,1)}) fusion(bf16[1,2,1024,2048]{3,2,1,0:T(8,128)(2,1)} %param.19, s32[]{:T(128)S(6)} %select_n.79), kind=kLoop, calls=%fused_computation.100 | loop fusion | bytes 16777220 | tf_op jit(solution)/shard_map/jit(dynamic_index_in_dim)/squeeze | solution.py:38
  15.1 4.2 dynamic-slice_bitcast_fusion
  19.6 400.0 %while.17 = (s32[]{:T(128)}, bf16[128,1024]{1,0:T(8,128)(2,1)S(1)}, bf16[2,128,1024]{2,1,0:T(8,128)(2,1)S(1)}, pred[]{:T(512)}, s32[]{:T(128)}, /*index=5*/bf16[...) while((s32[]{:T(128)}, bf16[128,1024]{1,0:T(8,128)(2,1)S(1)}, ...), condition=%wide.region_10.11_spmd.clone, body=%wide.region_0.10_spmd.clone.sunk | while | flops 3307674112 | bytes 38492604 | solution.py:119
  21.8 7.6 %all-to-all-start = ((bf16[16,2,8,1024]{3,2,1,0:T(8,128)(2,1)}), bf16[16,2,8,1024]{3,2,1,0:T(8,128)(2,1)S(1)}, u32[]{:S(2)}, u32[]{:S(2)}) async-start(bf16[16,2,8,1024]{3,2,1,0:T(8,128)(2,1)} %bitcast.90), calls=%async_computation | async-start | bytes 1048576 | tf_op jit(solution)/shard_map/while/body/eval_jaxpr/all_to_all | solution.py:100
  29.4 10.4 %all-to-all-done = bf16[16,2,8,1024]{3,2,1,0:T(8,128)(2,1)S(1)} async-done(((bf16[16,2,8,1024]{3,2,1,0:T(8,128)(2,1)}), bf16[16,2,8,1024]{3,2,1,0:T(8,128)(2,1)S(1)}, u32[]{:S(2)}, u32[]{:S(2)}) %all-to-all-start) | async-done | bytes 524320 | tf_op jit(solution)/shard_map/while/body/eval_jaxpr/all_to_all | solution.py:100
  40.7 3.6 all-to-all-start.1
  44.7 8.6 %all-to-all-done.1 = bf16[16,2,8,1024]{3,2,1,0:T(8,128)(2,1)S(1)} async-done(((bf16[16,2,8,1024]{3,2,1,0:T(8,128)(2,1)}), bf16[16,2,8,1024]{3,2,1,0:T(8,128)(2,1)S(1)}, u32[]{:S(2)}, u32[]{:S(2)}) %all-to-all-start.1) | async-done | bytes 524320 | tf_op jit(solution)/shard_map/while/body/eval_jaxpr/all_to_all | solution.py:102
  54.3 7.0 %collective-permute-start = (bf16[128,1024]{1,0:T(8,128)(2,1)S(1)}, bf16[128,1024]{1,0:T(8,128)(2,1)S(1)}, u32[]{:S(2)}, u32[]{:S(2)}) collective-permute-start(bf16[128,1024]{1,0:T(8,128)(2,1)S(1)} %get-tuple-element.555), channel_id=1, source_target_pairs={{0,16},{16,32},{32,48},{48,64},{64,80},{80,96},{96,112},{1,17},{17... | collective-permute-start | bytes 786440 | tf_op jit(solution)/shard_map/while/body/eval_jaxpr/ppermute | solution.py:10
  61.3 8.5 %collective-permute-done = bf16[128,1024]{1,0:T(8,128)(2,1)S(1)} collective-permute-done((bf16[128,1024]{1,0:T(8,128)(2,1)S(1)}, bf16[128,1024]{1,0:T(8,128)(2,1)S(1)}, u32[]{:S(2)}, u32[]{:S(2)}) %collective-permute-start) | collective-permute-done | bytes 262176 | tf_op jit(solution)/shard_map/while/body/eval_jaxpr/ppermute | solution.py:10
  72.0 3.6 all-to-all-start
  75.6 11.2 %all-to-all-done = bf16[16,2,8,1024]{3,2,1,0:T(8,128)(2,1)S(1)} async-done(((bf16[16,2,8,1024]{3,2,1,0:T(8,128)(2,1)}), bf16[16,2,8,1024]{3,2,1,0:T(8,128)(2,1)S(1)}, u32[]{:S(2)}, u32[]{:S(2)}) %all-to-all-start) | async-done | bytes 524320 | tf_op jit(solution)/shard_map/while/body/eval_jaxpr/all_to_all | solution.py:100
  86.7 10.1 %conditional.6 = (bf16[16,2,8,1024]{3,2,0,1:T(8,128)(2,1)S(1)}) conditional(s32[]{:T(128)} %convert_element_type.136, () %tuple.63, (bf16[16,2,8,1024]{3,2,1,0:T(8,128)(2,1)S(1)}, bf16[1024,2048]{1,0:T(8,128)(2,1)}, bf16[2048,1024]{1,0:T(8,128)(2,1)}, bf16[1024,2048]{1,0:T(8,128)(2,1)}, bf16[2048,1024]{1,0:T(8,128)(2,1)}) %tuple.64), branch_computations={%region_8.8_spmd, %region_9.9_spmd} | conditional | flops 2152726528 | bytes 18874376 | solution.py:96
  86.7 5.0 %fusion.22 = bf16[16,1,8,1024]{3,2,0,1:T(8,128)(2,1)S(1)} fusion(bf16[2048,1024]{1,0:T(8,128)(2,1)} %get-tuple-element.353, bf16[1024,2048]{1,0:T(8,128)(2,1)} %get-tuple-element.352, bf16[16,2,8,1024]{3,2,1,0:T(8,128)(2,1)S(1)} %get-tuple-element.351), kind=kOutput, calls=%fused_computation.25 | convolution fusion | flops 1076232192 | bytes 8912896 | tf_op jit(solution)/shard_map/while/body/eval_jaxpr/cond/branch_1_fun/dot_general | solution.py:21
  91.7 5.0 %fusion.23 = bf16[16,1,8,1024]{3,2,0,1:T(8,128)(2,1)S(1)} fusion(bf16[2048,1024]{1,0:T(8,128)(2,1)} %get-tuple-element.355, bf16[1024,2048]{1,0:T(8,128)(2,1)} %get-tuple-element.354, bf16[16,2,8,1024]{3,2,1,0:T(8,128)(2,1)S(1)} %get-tuple-element.351), kind=kOutput, calls=%fused_computation.26 | convolution fusion | flops 1076232192 | bytes 8912896 | tf_op jit(solution)/shard_map/while/body/eval_jaxpr/cond/branch_1_fun/dot_general | solution.py:21
  97.7 3.6 all-to-all-start.1
  101.3 5.0 %conditional.7 = (f32[128,1024]{1,0:T(8,128)S(1)}) conditional(s32[]{:T(128)} %convert_element_type.136, () %tuple.65, (bf16[128,1024]{1,0:T(8,128)(2,1)S(1)}, bf16[1024,2048]{1,0:T(8,128)(2,1)}, bf16[2048,1024]{1,0:T(8,128)(2,1)}) %tuple.66), branch_computations={%region_3.3_spmd, %region_4.4_spmd} | conditional | flops 1076101120 | bytes 9175048 | solution.py:103
  101.3 5.0 %fusion.12 = f32[128,1024]{1,0:T(8,128)S(1)} fusion(bf16[2048,1024]{1,0:T(8,128)(2,1)} %get-tuple-element.350, bf16[128,1024]{1,0:T(8,128)(2,1)S(1)} %get-tuple-element.348, bf16[1024,2048]{1,0:T(8,128)(2,1)} %get-tuple-element.349), kind=kOutput, calls=%fused_computation.12 | convolution fusion | flops 1076101120 | bytes 9175040 | tf_op jit(solution)/shard_map/while/body/eval_jaxpr/cond/branch_1_fun/dot_general | solution.py:63
  106.6 5.0 %all-to-all-done.1 = bf16[16,2,8,1024]{3,2,1,0:T(8,128)(2,1)S(1)} async-done(((bf16[16,2,8,1024]{3,2,1,0:T(8,128)(2,1)}), bf16[16,2,8,1024]{3,2,1,0:T(8,128)(2,1)S(1)}, u32[]{:S(2)}, u32[]{:S(2)}) %all-to-all-start.1) | async-done | bytes 524320 | tf_op jit(solution)/shard_map/while/body/eval_jaxpr/all_to_all | solution.py:102
  114.6 3.3 collective-permute-done
  120.0 3.6 all-to-all-start
  123.6 11.7 %all-to-all-done = bf16[16,2,8,1024]{3,2,1,0:T(8,128)(2,1)S(1)} async-done(((bf16[16,2,8,1024]{3,2,1,0:T(8,128)(2,1)}), bf16[16,2,8,1024]{3,2,1,0:T(8,128)(2,1)S(1)}, u32[]{:S(2)}, u32[]{:S(2)}) %all-to-all-start) | async-done | bytes 524320 | tf_op jit(solution)/shard_map/while/body/eval_jaxpr/all_to_all | solution.py:100
  135.3 10.1 %conditional.6 = (bf16[16,2,8,1024]{3,2,0,1:T(8,128)(2,1)S(1)}) conditional(s32[]{:T(128)} %convert_element_type.136, () %tuple.63, (bf16[16,2,8,1024]{3,2,1,0:T(8,128)(2,1)S(1)}, bf16[1024,2048]{1,0:T(8,128)(2,1)}, bf16[2048,1024]{1,0:T(8,128)(2,1)}, bf16[1024,2048]{1,0:T(8,128)(2,1)}, bf16[2048,1024]{1,0:T(8,128)(2,1)}) %tuple.64), branch_computations={%region_8.8_spmd, %region_9.9_spmd} | conditional | flops 2152726528 | bytes 18874376 | solution.py:96
  135.3 5.0 %fusion.22 = bf16[16,1,8,1024]{3,2,0,1:T(8,128)(2,1)S(1)} fusion(bf16[2048,1024]{1,0:T(8,128)(2,1)} %get-tuple-element.353, bf16[1024,2048]{1,0:T(8,128)(2,1)} %get-tuple-element.352, bf16[16,2,8,1024]{3,2,1,0:T(8,128)(2,1)S(1)} %get-tuple-element.351), kind=kOutput, calls=%fused_computation.25 | convolution fusion | flops 1076232192 | bytes 8912896 | tf_op jit(solution)/shard_map/while/body/eval_jaxpr/cond/branch_1_fun/dot_general | solution.py:21
  140.4 5.0 %fusion.23 = bf16[16,1,8,1024]{3,2,0,1:T(8,128)(2,1)S(1)} fusion(bf16[2048,1024]{1,0:T(8,128)(2,1)} %get-tuple-element.355, bf16[1024,2048]{1,0:T(8,128)(2,1)} %get-tuple-element.354, bf16[16,2,8,1024]{3,2,1,0:T(8,128)(2,1)S(1)} %get-tuple-element.351), kind=kOutput, calls=%fused_computation.26 | convolution fusion | flops 1076232192 | bytes 8912896 | tf_op jit(solution)/shard_map/while/body/eval_jaxpr/cond/branch_1_fun/dot_general | solution.py:21
  146.3 3.6 all-to-all-start.1
  149.9 5.0 %conditional.7 = (f32[128,1024]{1,0:T(8,128)S(1)}) conditional(s32[]{:T(128)} %convert_element_type.136, () %tuple.65, (bf16[128,1024]{1,0:T(8,128)(2,1)S(1)}, bf16[1024,2048]{1,0:T(8,128)(2,1)}, bf16[2048,1024]{1,0:T(8,128)(2,1)}) %tuple.66), branch_computations={%region_3.3_spmd, %region_4.4_spmd} | conditional | flops 1076101120 | bytes 9175048 | solution.py:103
  149.9 5.0 %fusion.12 = f32[128,1024]{1,0:T(8,128)S(1)} fusion(bf16[2048,1024]{1,0:T(8,128)(2,1)} %get-tuple-element.350, bf16[128,1024]{1,0:T(8,128)(2,1)S(1)} %get-tuple-element.348, bf16[1024,2048]{1,0:T(8,128)(2,1)} %get-tuple-element.349), kind=kOutput, calls=%fused_computation.12 | convolution fusion | flops 1076101120 | bytes 9175040 | tf_op jit(solution)/shard_map/while/body/eval_jaxpr/cond/branch_1_fun/dot_general | solution.py:63
  155.2 3.6 all-to-all-done.1
  159.9 6.1 %collective-permute-start = (bf16[128,1024]{1,0:T(8,128)(2,1)S(1)}, bf16[128,1024]{1,0:T(8,128)(2,1)S(1)}, u32[]{:S(2)}, u32[]{:S(2)}) collective-permute-start(bf16[128,1024]{1,0:T(8,128)(2,1)S(1)} %get-tuple-element.555), channel_id=1, source_target_pairs={{0,16},{16,32},{32,48},{48,64},{64,80},{80,96},{96,112},{1,17},{17... | collective-permute-start | bytes 786440 | tf_op jit(solution)/shard_map/while/body/eval_jaxpr/ppermute | solution.py:10
  171.4 3.6 all-to-all-start
  175.0 8.9 %all-to-all-done = bf16[16,2,8,1024]{3,2,1,0:T(8,128)(2,1)S(1)} async-done(((bf16[16,2,8,1024]{3,2,1,0:T(8,128)(2,1)}), bf16[16,2,8,1024]{3,2,1,0:T(8,128)(2,1)S(1)}, u32[]{:S(2)}, u32[]{:S(2)}) %all-to-all-start) | async-done | bytes 524320 | tf_op jit(solution)/shard_map/while/body/eval_jaxpr/all_to_all | solution.py:100
  184.8 3.6 all-to-all-start.1
  188.8 8.6 %all-to-all-done.1 = bf16[16,2,8,1024]{3,2,1,0:T(8,128)(2,1)S(1)} async-done(((bf16[16,2,8,1024]{3,2,1,0:T(8,128)(2,1)}), bf16[16,2,8,1024]{3,2,1,0:T(8,128)(2,1)S(1)}, u32[]{:S(2)}, u32[]{:S(2)}) %all-to-all-start.1) | async-done | bytes 524320 | tf_op jit(solution)/shard_map/while/body/eval_jaxpr/all_to_all | solution.py:102
  198.4 16.7 %collective-permute-start = (bf16[128,1024]{1,0:T(8,128)(2,1)S(1)}, bf16[128,1024]{1,0:T(8,128)(2,1)S(1)}, u32[]{:S(2)}, u32[]{:S(2)}) collective-permute-start(bf16[128,1024]{1,0:T(8,128)(2,1)S(1)} %get-tuple-element.555), channel_id=1, source_target_pairs={{0,16},{16,32},{32,48},{48,64},{64,80},{80,96},{96,112},{1,17},{17... | collective-permute-start | bytes 786440 | tf_op jit(solution)/shard_map/while/body/eval_jaxpr/ppermute | solution.py:10
  215.1 3.3 collective-permute-done
  220.6 3.6 all-to-all-start
  224.2 10.4 %all-to-all-done = bf16[16,2,8,1024]{3,2,1,0:T(8,128)(2,1)S(1)} async-done(((bf16[16,2,8,1024]{3,2,1,0:T(8,128)(2,1)}), bf16[16,2,8,1024]{3,2,1,0:T(8,128)(2,1)S(1)}, u32[]{:S(2)}, u32[]{:S(2)}) %all-to-all-start) | async-done | bytes 524320 | tf_op jit(solution)/shard_map/while/body/eval_jaxpr/all_to_all | solution.py:100
  235.5 3.6 all-to-all-start.1
  239.4 8.6 %all-to-all-done.1 = bf16[16,2,8,1024]{3,2,1,0:T(8,128)(2,1)S(1)} async-done(((bf16[16,2,8,1024]{3,2,1,0:T(8,128)(2,1)}), bf16[16,2,8,1024]{3,2,1,0:T(8,128)(2,1)S(1)}, u32[]{:S(2)}, u32[]{:S(2)}) %all-to-all-start.1) | async-done | bytes 524320 | tf_op jit(solution)/shard_map/while/body/eval_jaxpr/all_to_all | solution.py:102
  249.1 5.2 %collective-permute-start = (bf16[128,1024]{1,0:T(8,128)(2,1)S(1)}, bf16[128,1024]{1,0:T(8,128)(2,1)S(1)}, u32[]{:S(2)}, u32[]{:S(2)}) collective-permute-start(bf16[128,1024]{1,0:T(8,128)(2,1)S(1)} %get-tuple-element.555), channel_id=1, source_target_pairs={{0,16},{16,32},{32,48},{48,64},{64,80},{80,96},{96,112},{1,17},{17... | collective-permute-start | bytes 786440 | tf_op jit(solution)/shard_map/while/body/eval_jaxpr/ppermute | solution.py:10
  254.3 3.3 collective-permute-done
  259.8 3.6 all-to-all-start
  263.3 8.9 %all-to-all-done = bf16[16,2,8,1024]{3,2,1,0:T(8,128)(2,1)S(1)} async-done(((bf16[16,2,8,1024]{3,2,1,0:T(8,128)(2,1)}), bf16[16,2,8,1024]{3,2,1,0:T(8,128)(2,1)S(1)}, u32[]{:S(2)}, u32[]{:S(2)}) %all-to-all-start) | async-done | bytes 524320 | tf_op jit(solution)/shard_map/while/body/eval_jaxpr/all_to_all | solution.py:100
  273.2 3.6 all-to-all-start.1
  277.2 8.6 %all-to-all-done.1 = bf16[16,2,8,1024]{3,2,1,0:T(8,128)(2,1)S(1)} async-done(((bf16[16,2,8,1024]{3,2,1,0:T(8,128)(2,1)}), bf16[16,2,8,1024]{3,2,1,0:T(8,128)(2,1)S(1)}, u32[]{:S(2)}, u32[]{:S(2)}) %all-to-all-start.1) | async-done | bytes 524320 | tf_op jit(solution)/shard_map/while/body/eval_jaxpr/all_to_all | solution.py:102
  286.8 11.8 %collective-permute-start = (bf16[128,1024]{1,0:T(8,128)(2,1)S(1)}, bf16[128,1024]{1,0:T(8,128)(2,1)S(1)}, u32[]{:S(2)}, u32[]{:S(2)}) collective-permute-start(bf16[128,1024]{1,0:T(8,128)(2,1)S(1)} %get-tuple-element.555), channel_id=1, source_target_pairs={{0,16},{16,32},{32,48},{48,64},{64,80},{80,96},{96,112},{1,17},{17... | collective-permute-start | bytes 786440 | tf_op jit(solution)/shard_map/while/body/eval_jaxpr/ppermute | solution.py:10
  304.0 3.6 all-to-all-start
  307.6 8.9 %all-to-all-done = bf16[16,2,8,1024]{3,2,1,0:T(8,128)(2,1)S(1)} async-done(((bf16[16,2,8,1024]{3,2,1,0:T(8,128)(2,1)}), bf16[16,2,8,1024]{3,2,1,0:T(8,128)(2,1)S(1)}, u32[]{:S(2)}, u32[]{:S(2)}) %all-to-all-start) | async-done | bytes 524320 | tf_op jit(solution)/shard_map/while/body/eval_jaxpr/all_to_all | solution.py:100
  317.5 3.6 all-to-all-start.1
  321.4 8.6 %all-to-all-done.1 = bf16[16,2,8,1024]{3,2,1,0:T(8,128)(2,1)S(1)} async-done(((bf16[16,2,8,1024]{3,2,1,0:T(8,128)(2,1)}), bf16[16,2,8,1024]{3,2,1,0:T(8,128)(2,1)S(1)}, u32[]{:S(2)}, u32[]{:S(2)}) %all-to-all-start.1) | async-done | bytes 524320 | tf_op jit(solution)/shard_map/while/body/eval_jaxpr/all_to_all | solution.py:102
  331.1 6.7 %collective-permute-start = (bf16[128,1024]{1,0:T(8,128)(2,1)S(1)}, bf16[128,1024]{1,0:T(8,128)(2,1)S(1)}, u32[]{:S(2)}, u32[]{:S(2)}) collective-permute-start(bf16[128,1024]{1,0:T(8,128)(2,1)S(1)} %get-tuple-element.555), channel_id=1, source_target_pairs={{0,16},{16,32},{32,48},{48,64},{64,80},{80,96},{96,112},{1,17},{17... | collective-permute-start | bytes 786440 | tf_op jit(solution)/shard_map/while/body/eval_jaxpr/ppermute | solution.py:10
  343.2 3.6 all-to-all-start
  346.8 8.9 %all-to-all-done = bf16[16,2,8,1024]{3,2,1,0:T(8,128)(2,1)S(1)} async-done(((bf16[16,2,8,1024]{3,2,1,0:T(8,128)(2,1)}), bf16[16,2,8,1024]{3,2,1,0:T(8,128)(2,1)S(1)}, u32[]{:S(2)}, u32[]{:S(2)}) %all-to-all-start) | async-done | bytes 524320 | tf_op jit(solution)/shard_map/while/body/eval_jaxpr/all_to_all | solution.py:100
  356.7 3.6 all-to-all-start.1
  360.7 8.6 %all-to-all-done.1 = bf16[16,2,8,1024]{3,2,1,0:T(8,128)(2,1)S(1)} async-done(((bf16[16,2,8,1024]{3,2,1,0:T(8,128)(2,1)}), bf16[16,2,8,1024]{3,2,1,0:T(8,128)(2,1)S(1)}, u32[]{:S(2)}, u32[]{:S(2)}) %all-to-all-start.1) | async-done | bytes 524320 | tf_op jit(solution)/shard_map/while/body/eval_jaxpr/all_to_all | solution.py:102
  370.3 6.8 %collective-permute-start = (bf16[128,1024]{1,0:T(8,128)(2,1)S(1)}, bf16[128,1024]{1,0:T(8,128)(2,1)S(1)}, u32[]{:S(2)}, u32[]{:S(2)}) collective-permute-start(bf16[128,1024]{1,0:T(8,128)(2,1)S(1)} %get-tuple-element.555), channel_id=1, source_target_pairs={{0,16},{16,32},{32,48},{48,64},{64,80},{80,96},{96,112},{1,17},{17... | collective-permute-start | bytes 786440 | tf_op jit(solution)/shard_map/while/body/eval_jaxpr/ppermute | solution.py:10
  377.1 3.3 collective-permute-done
  382.5 3.6 all-to-all-start
  386.1 8.9 %all-to-all-done = bf16[16,2,8,1024]{3,2,1,0:T(8,128)(2,1)S(1)} async-done(((bf16[16,2,8,1024]{3,2,1,0:T(8,128)(2,1)}), bf16[16,2,8,1024]{3,2,1,0:T(8,128)(2,1)S(1)}, u32[]{:S(2)}, u32[]{:S(2)}) %all-to-all-start) | async-done | bytes 524320 | tf_op jit(solution)/shard_map/while/body/eval_jaxpr/all_to_all | solution.py:100
  396.0 3.6 all-to-all-start.1
  399.9 8.6 %all-to-all-done.1 = bf16[16,2,8,1024]{3,2,1,0:T(8,128)(2,1)S(1)} async-done(((bf16[16,2,8,1024]{3,2,1,0:T(8,128)(2,1)}), bf16[16,2,8,1024]{3,2,1,0:T(8,128)(2,1)S(1)}, u32[]{:S(2)}, u32[]{:S(2)}) %all-to-all-start.1) | async-done | bytes 524320 | tf_op jit(solution)/shard_map/while/body/eval_jaxpr/all_to_all | solution.py:102
  409.6 6.7 %collective-permute-start = (bf16[128,1024]{1,0:T(8,128)(2,1)S(1)}, bf16[128,1024]{1,0:T(8,128)(2,1)S(1)}, u32[]{:S(2)}, u32[]{:S(2)}) collective-permute-start(bf16[128,1024]{1,0:T(8,128)(2,1)S(1)} %get-tuple-element.555), channel_id=1, source_target_pairs={{0,16},{16,32},{32,48},{48,64},{64,80},{80,96},{96,112},{1,17},{17... | collective-permute-start | bytes 786440 | tf_op jit(solution)/shard_map/while/body/eval_jaxpr/ppermute | solution.py:10
  416.3 3.3 collective-permute-done
  420.4 49.6 %all-gather.3.cloned.1.call-done = bf16[16,128,1024]{2,1,0:T(8,128)(2,1)} async-done(((bf16[2,128,1024]{2,1,0:T(8,128)(2,1)}), bf16[16,128,1024]{2,1,0:T(8,128)(2,1)}) %all-gather.3.cloned.1.call-update) | async-done | bytes 4194320 | tf_op jit(solution)/shard_map/all_gather | solution.py:14
  (233 shorter events, 54.8 us)
Async XLA Ops:
  6.5 463.4 %all-gather.3.cloned.1.call-start = ((), (), s32[]{:S(2)}) async-start(), calls=%async_computation.2 | async-start | bytes 4718592 | tf_op jit(solution)/shard_map/all_gather | solution.py:14
  6.5 8.5 %copy-start.1 = (bf16[1,2,2048,1024]{3,2,1,0:T(8,128)(2,1)S(1)}, bf16[1,2,2048,1024]{3,2,1,0:T(8,128)(2,1)}, u32[]{:S(2)}) copy-start(bf16[1,2,2048,1024]{3,2,1,0:T(8,128)(2,1)} %param.20) | copy-start | bytes 25165828
  15.0 4.3 copy-start.4
  15.0 4.5 copy-start.2
  15.0 4.5 copy-start.3
  15.1 4.5 copy-start.5
  21.8 18.0 %all-to-all-start = ((bf16[16,2,8,1024]{3,2,1,0:T(8,128)(2,1)}), bf16[16,2,8,1024]{3,2,1,0:T(8,128)(2,1)S(1)}, u32[]{:S(2)}, u32[]{:S(2)}) async-start(bf16[16,2,8,1024]{3,2,1,0:T(8,128)(2,1)} %bitcast.90), calls=%async_computation | async-start | bytes 1048576 | tf_op jit(solution)/shard_map/while/body/eval_jaxpr/all_to_all | solution.py:100
  40.7 12.5 %all-to-all-start.1 = ((bf16[16,2,8,1024]{3,2,1,0:T(8,128)(2,1)}), bf16[16,2,8,1024]{3,2,1,0:T(8,128)(2,1)S(1)}, u32[]{:S(2)}, u32[]{:S(2)}) async-start(bf16[16,2,8,1024]{3,2,1,0:T(8,128)(2,1)} %copy.22), calls=%async_computation.1 | async-start | bytes 1048576 | tf_op jit(solution)/shard_map/while/body/eval_jaxpr/all_to_all | solution.py:102
  54.3 15.5 %collective-permute-start = (bf16[128,1024]{1,0:T(8,128)(2,1)S(1)}, bf16[128,1024]{1,0:T(8,128)(2,1)S(1)}, u32[]{:S(2)}, u32[]{:S(2)}) collective-permute-start(bf16[128,1024]{1,0:T(8,128)(2,1)S(1)} %get-tuple-element.555), channel_id=1, source_target_pairs={{0,16},{16,32},{32,48},{48,64},{64,80},{80,96},{96,112},{1,17},{17... | collective-permute-start | bytes 786440 | tf_op jit(solution)/shard_map/while/body/eval_jaxpr/ppermute | solution.py:10
  72.0 14.7 %all-to-all-start = ((bf16[16,2,8,1024]{3,2,1,0:T(8,128)(2,1)}), bf16[16,2,8,1024]{3,2,1,0:T(8,128)(2,1)S(1)}, u32[]{:S(2)}, u32[]{:S(2)}) async-start(bf16[16,2,8,1024]{3,2,1,0:T(8,128)(2,1)} %bitcast.90), calls=%async_computation | async-start | bytes 1048576 | tf_op jit(solution)/shard_map/while/body/eval_jaxpr/all_to_all | solution.py:100
  97.7 13.9 %all-to-all-start.1 = ((bf16[16,2,8,1024]{3,2,1,0:T(8,128)(2,1)}), bf16[16,2,8,1024]{3,2,1,0:T(8,128)(2,1)S(1)}, u32[]{:S(2)}, u32[]{:S(2)}) async-start(bf16[16,2,8,1024]{3,2,1,0:T(8,128)(2,1)} %copy.22), calls=%async_computation.1 | async-start | bytes 1048576 | tf_op jit(solution)/shard_map/while/body/eval_jaxpr/all_to_all | solution.py:102
  112.6 5.2 %collective-permute-start = (bf16[128,1024]{1,0:T(8,128)(2,1)S(1)}, bf16[128,1024]{1,0:T(8,128)(2,1)S(1)}, u32[]{:S(2)}, u32[]{:S(2)}) collective-permute-start(bf16[128,1024]{1,0:T(8,128)(2,1)S(1)} %get-tuple-element.555), channel_id=1, source_target_pairs={{0,16},{16,32},{32,48},{48,64},{64,80},{80,96},{96,112},{1,17},{17... | collective-permute-start | bytes 786440 | tf_op jit(solution)/shard_map/while/body/eval_jaxpr/ppermute | solution.py:10
  120.0 15.3 %all-to-all-start = ((bf16[16,2,8,1024]{3,2,1,0:T(8,128)(2,1)}), bf16[16,2,8,1024]{3,2,1,0:T(8,128)(2,1)S(1)}, u32[]{:S(2)}, u32[]{:S(2)}) async-start(bf16[16,2,8,1024]{3,2,1,0:T(8,128)(2,1)} %bitcast.90), calls=%async_computation | async-start | bytes 1048576 | tf_op jit(solution)/shard_map/while/body/eval_jaxpr/all_to_all | solution.py:100
  146.3 12.5 %all-to-all-start.1 = ((bf16[16,2,8,1024]{3,2,1,0:T(8,128)(2,1)}), bf16[16,2,8,1024]{3,2,1,0:T(8,128)(2,1)S(1)}, u32[]{:S(2)}, u32[]{:S(2)}) async-start(bf16[16,2,8,1024]{3,2,1,0:T(8,128)(2,1)} %copy.22), calls=%async_computation.1 | async-start | bytes 1048576 | tf_op jit(solution)/shard_map/while/body/eval_jaxpr/all_to_all | solution.py:102
  159.9 9.4 %collective-permute-start = (bf16[128,1024]{1,0:T(8,128)(2,1)S(1)}, bf16[128,1024]{1,0:T(8,128)(2,1)S(1)}, u32[]{:S(2)}, u32[]{:S(2)}) collective-permute-start(bf16[128,1024]{1,0:T(8,128)(2,1)S(1)} %get-tuple-element.555), channel_id=1, source_target_pairs={{0,16},{16,32},{32,48},{48,64},{64,80},{80,96},{96,112},{1,17},{17... | collective-permute-start | bytes 786440 | tf_op jit(solution)/shard_map/while/body/eval_jaxpr/ppermute | solution.py:10
  171.4 12.5 %all-to-all-start = ((bf16[16,2,8,1024]{3,2,1,0:T(8,128)(2,1)}), bf16[16,2,8,1024]{3,2,1,0:T(8,128)(2,1)S(1)}, u32[]{:S(2)}, u32[]{:S(2)}) async-start(bf16[16,2,8,1024]{3,2,1,0:T(8,128)(2,1)} %bitcast.90), calls=%async_computation | async-start | bytes 1048576 | tf_op jit(solution)/shard_map/while/body/eval_jaxpr/all_to_all | solution.py:100
  184.8 12.5 %all-to-all-start.1 = ((bf16[16,2,8,1024]{3,2,1,0:T(8,128)(2,1)}), bf16[16,2,8,1024]{3,2,1,0:T(8,128)(2,1)S(1)}, u32[]{:S(2)}, u32[]{:S(2)}) async-start(bf16[16,2,8,1024]{3,2,1,0:T(8,128)(2,1)} %copy.22), calls=%async_computation.1 | async-start | bytes 1048576 | tf_op jit(solution)/shard_map/while/body/eval_jaxpr/all_to_all | solution.py:102
  198.4 20.0 %collective-permute-start = (bf16[128,1024]{1,0:T(8,128)(2,1)S(1)}, bf16[128,1024]{1,0:T(8,128)(2,1)S(1)}, u32[]{:S(2)}, u32[]{:S(2)}) collective-permute-start(bf16[128,1024]{1,0:T(8,128)(2,1)S(1)} %get-tuple-element.555), channel_id=1, source_target_pairs={{0,16},{16,32},{32,48},{48,64},{64,80},{80,96},{96,112},{1,17},{17... | collective-permute-start | bytes 786440 | tf_op jit(solution)/shard_map/while/body/eval_jaxpr/ppermute | solution.py:10
  220.6 14.0 %all-to-all-start = ((bf16[16,2,8,1024]{3,2,1,0:T(8,128)(2,1)}), bf16[16,2,8,1024]{3,2,1,0:T(8,128)(2,1)S(1)}, u32[]{:S(2)}, u32[]{:S(2)}) async-start(bf16[16,2,8,1024]{3,2,1,0:T(8,128)(2,1)} %bitcast.90), calls=%async_computation | async-start | bytes 1048576 | tf_op jit(solution)/shard_map/while/body/eval_jaxpr/all_to_all | solution.py:100
  235.5 12.5 %all-to-all-start.1 = ((bf16[16,2,8,1024]{3,2,1,0:T(8,128)(2,1)}), bf16[16,2,8,1024]{3,2,1,0:T(8,128)(2,1)S(1)}, u32[]{:S(2)}, u32[]{:S(2)}) async-start(bf16[16,2,8,1024]{3,2,1,0:T(8,128)(2,1)} %copy.22), calls=%async_computation.1 | async-start | bytes 1048576 | tf_op jit(solution)/shard_map/while/body/eval_jaxpr/all_to_all | solution.py:102
  249.1 8.6 %collective-permute-start = (bf16[128,1024]{1,0:T(8,128)(2,1)S(1)}, bf16[128,1024]{1,0:T(8,128)(2,1)S(1)}, u32[]{:S(2)}, u32[]{:S(2)}) collective-permute-start(bf16[128,1024]{1,0:T(8,128)(2,1)S(1)} %get-tuple-element.555), channel_id=1, source_target_pairs={{0,16},{16,32},{32,48},{48,64},{64,80},{80,96},{96,112},{1,17},{17... | collective-permute-start | bytes 786440 | tf_op jit(solution)/shard_map/while/body/eval_jaxpr/ppermute | solution.py:10
  259.8 12.5 %all-to-all-start = ((bf16[16,2,8,1024]{3,2,1,0:T(8,128)(2,1)}), bf16[16,2,8,1024]{3,2,1,0:T(8,128)(2,1)S(1)}, u32[]{:S(2)}, u32[]{:S(2)}) async-start(bf16[16,2,8,1024]{3,2,1,0:T(8,128)(2,1)} %bitcast.90), calls=%async_computation | async-start | bytes 1048576 | tf_op jit(solution)/shard_map/while/body/eval_jaxpr/all_to_all | solution.py:100
  273.2 12.5 %all-to-all-start.1 = ((bf16[16,2,8,1024]{3,2,1,0:T(8,128)(2,1)}), bf16[16,2,8,1024]{3,2,1,0:T(8,128)(2,1)S(1)}, u32[]{:S(2)}, u32[]{:S(2)}) async-start(bf16[16,2,8,1024]{3,2,1,0:T(8,128)(2,1)} %copy.22), calls=%async_computation.1 | async-start | bytes 1048576 | tf_op jit(solution)/shard_map/while/body/eval_jaxpr/all_to_all | solution.py:102
  286.8 15.1 %collective-permute-start = (bf16[128,1024]{1,0:T(8,128)(2,1)S(1)}, bf16[128,1024]{1,0:T(8,128)(2,1)S(1)}, u32[]{:S(2)}, u32[]{:S(2)}) collective-permute-start(bf16[128,1024]{1,0:T(8,128)(2,1)S(1)} %get-tuple-element.555), channel_id=1, source_target_pairs={{0,16},{16,32},{32,48},{48,64},{64,80},{80,96},{96,112},{1,17},{17... | collective-permute-start | bytes 786440 | tf_op jit(solution)/shard_map/while/body/eval_jaxpr/ppermute | solution.py:10
  304.0 12.5 %all-to-all-start = ((bf16[16,2,8,1024]{3,2,1,0:T(8,128)(2,1)}), bf16[16,2,8,1024]{3,2,1,0:T(8,128)(2,1)S(1)}, u32[]{:S(2)}, u32[]{:S(2)}) async-start(bf16[16,2,8,1024]{3,2,1,0:T(8,128)(2,1)} %bitcast.90), calls=%async_computation | async-start | bytes 1048576 | tf_op jit(solution)/shard_map/while/body/eval_jaxpr/all_to_all | solution.py:100
  317.5 12.5 %all-to-all-start.1 = ((bf16[16,2,8,1024]{3,2,1,0:T(8,128)(2,1)}), bf16[16,2,8,1024]{3,2,1,0:T(8,128)(2,1)S(1)}, u32[]{:S(2)}, u32[]{:S(2)}) async-start(bf16[16,2,8,1024]{3,2,1,0:T(8,128)(2,1)} %copy.22), calls=%async_computation.1 | async-start | bytes 1048576 | tf_op jit(solution)/shard_map/while/body/eval_jaxpr/all_to_all | solution.py:102
  331.1 10.0 %collective-permute-start = (bf16[128,1024]{1,0:T(8,128)(2,1)S(1)}, bf16[128,1024]{1,0:T(8,128)(2,1)S(1)}, u32[]{:S(2)}, u32[]{:S(2)}) collective-permute-start(bf16[128,1024]{1,0:T(8,128)(2,1)S(1)} %get-tuple-element.555), channel_id=1, source_target_pairs={{0,16},{16,32},{32,48},{48,64},{64,80},{80,96},{96,112},{1,17},{17... | collective-permute-start | bytes 786440 | tf_op jit(solution)/shard_map/while/body/eval_jaxpr/ppermute | solution.py:10
  343.2 12.5 %all-to-all-start = ((bf16[16,2,8,1024]{3,2,1,0:T(8,128)(2,1)}), bf16[16,2,8,1024]{3,2,1,0:T(8,128)(2,1)S(1)}, u32[]{:S(2)}, u32[]{:S(2)}) async-start(bf16[16,2,8,1024]{3,2,1,0:T(8,128)(2,1)} %bitcast.90), calls=%async_computation | async-start | bytes 1048576 | tf_op jit(solution)/shard_map/while/body/eval_jaxpr/all_to_all | solution.py:100
  356.7 12.5 %all-to-all-start.1 = ((bf16[16,2,8,1024]{3,2,1,0:T(8,128)(2,1)}), bf16[16,2,8,1024]{3,2,1,0:T(8,128)(2,1)S(1)}, u32[]{:S(2)}, u32[]{:S(2)}) async-start(bf16[16,2,8,1024]{3,2,1,0:T(8,128)(2,1)} %copy.22), calls=%async_computation.1 | async-start | bytes 1048576 | tf_op jit(solution)/shard_map/while/body/eval_jaxpr/all_to_all | solution.py:102
  370.3 10.1 %collective-permute-start = (bf16[128,1024]{1,0:T(8,128)(2,1)S(1)}, bf16[128,1024]{1,0:T(8,128)(2,1)S(1)}, u32[]{:S(2)}, u32[]{:S(2)}) collective-permute-start(bf16[128,1024]{1,0:T(8,128)(2,1)S(1)} %get-tuple-element.555), channel_id=1, source_target_pairs={{0,16},{16,32},{32,48},{48,64},{64,80},{80,96},{96,112},{1,17},{17... | collective-permute-start | bytes 786440 | tf_op jit(solution)/shard_map/while/body/eval_jaxpr/ppermute | solution.py:10
  382.5 12.5 %all-to-all-start = ((bf16[16,2,8,1024]{3,2,1,0:T(8,128)(2,1)}), bf16[16,2,8,1024]{3,2,1,0:T(8,128)(2,1)S(1)}, u32[]{:S(2)}, u32[]{:S(2)}) async-start(bf16[16,2,8,1024]{3,2,1,0:T(8,128)(2,1)} %bitcast.90), calls=%async_computation | async-start | bytes 1048576 | tf_op jit(solution)/shard_map/while/body/eval_jaxpr/all_to_all | solution.py:100
  396.0 12.5 %all-to-all-start.1 = ((bf16[16,2,8,1024]{3,2,1,0:T(8,128)(2,1)}), bf16[16,2,8,1024]{3,2,1,0:T(8,128)(2,1)S(1)}, u32[]{:S(2)}, u32[]{:S(2)}) async-start(bf16[16,2,8,1024]{3,2,1,0:T(8,128)(2,1)} %copy.22), calls=%async_computation.1 | async-start | bytes 1048576 | tf_op jit(solution)/shard_map/while/body/eval_jaxpr/all_to_all | solution.py:102
  409.6 10.0 %collective-permute-start = (bf16[128,1024]{1,0:T(8,128)(2,1)S(1)}, bf16[128,1024]{1,0:T(8,128)(2,1)S(1)}, u32[]{:S(2)}, u32[]{:S(2)}) collective-permute-start(bf16[128,1024]{1,0:T(8,128)(2,1)S(1)} %get-tuple-element.555), channel_id=1, source_target_pairs={{0,16},{16,32},{32,48},{48,64},{64,80},{80,96},{96,112},{1,17},{17... | collective-permute-start | bytes 786440 | tf_op jit(solution)/shard_map/while/body/eval_jaxpr/ppermute | solution.py:10
  419.6 0.8 copy-start
Sparse Core Ops, SparseCore 0:
  420.5 49.3 all-gather.2
where the time goes:
time: 481 us; the launch traced here: 479 us
  waiting for transfers between devices  242 us (50%)
  starting transfers between devices  137 us (28%)
  matrix products  42.1 us (9%)
  local copies, waits for them, and re-layouts  33.1 us (7%)
  between operations  13.5 us (3%)
  other arithmetic  9.63 us (2%)
    all_to_all x9, waiting for transfers between devices, step(): lax.all_to_all(outgoing, 'expert', split_axis=0, concat_axis=0, tiled=True)  88.4 us
    ppermute x9, starting transfers between devices, passed_along(): lax.ppermute(value, axis, [(source, source + steps) for source in range(i...  68.9 us
    all_to_all x9, waiting for transfers between devices, step(): lax.all_to_all(expert_rows, 'expert', split_axis=0, concat_axis=0, tiled=...  68.7 us
    all_gather x1, waiting for transfers between devices, picked_2(): lax.all_gather(value, axis)  49.6 us
    all_to_all x9, starting transfers between devices, step(): lax.all_to_all(outgoing, 'expert', split_axis=0, concat_axis=0, tiled=True)  36.1 us
    ppermute x9, waiting for transfers between devices, passed_along(): lax.ppermute(value, axis, [(source, source + steps) for source in range(i...  34.9 us
    all_to_all x9, starting transfers between devices, step(): lax.all_to_all(expert_rows, 'expert', split_axis=0, concat_axis=0, tiled=...  32.1 us
    dot_general x4, matrix products, expert_mlp(): jnp.dot(activation, weight_out, preferred_element_type=jnp.float32)  20 us
  transfers between devices with their start and end apart: 28, of which 28 were waited for; matrix products, arithmetic and copies ran while one was open for 3% of the time, Pallas kernels for 0%

commit v1 on v0

v1 whole, which is shorter than its diff:
```python
import functools

import jax
import jax.numpy as jnp
from jax import lax
from jax.experimental import pallas as pl
from jax.experimental.pallas import tpu as pltpu
from jax.sharding import PartitionSpec as P

BF16 = jnp.bfloat16
F32 = jnp.float32
VMEM_SPEC = pl.BlockSpec(memory_space=pltpu.VMEM)
SMEM_SPEC = pl.BlockSpec(memory_space=pltpu.SMEM)
HBM_SPEC = pl.BlockSpec(memory_space=pl.ANY)
LIMIT = 30 << 20
PARTS = 4


def dot(a, b):
    return jnp.dot(a, b, preferred_element_type=F32)


def tables_kernel(ids_ref, send_ref, take_ref, picked_ref):
    blocks, tokens = ids_ref.shape
    slots = send_ref.shape[1]
    labels = picked_ref.shape[2]
    earlier = (
        lax.broadcasted_iota(jnp.int32, (tokens, tokens), 0)
        < lax.broadcasted_iota(jnp.int32, (tokens, tokens), 1)
    ).astype(BF16)
    capacity = slots // (labels // 4)
    for block in range(blocks):
        ids = ids_ref[block : block + 1, :]
        picked = (lax.broadcasted_iota(jnp.int32, (labels, tokens), 0) == ids).astype(F32)
        before = dot(picked.astype(BF16), earlier)
        position = jnp.sum(before * picked, axis=0, keepdims=True).astype(jnp.int32)
        slot = ids * capacity + position
        send = (lax.broadcasted_iota(jnp.int32, (slots, tokens), 0) == slot).astype(F32)
        send_ref[block] = send.astype(BF16)
        take_ref[block] = send.T.astype(BF16)
        picked_ref[block] = picked.T


def stream_of(info_ref, tokens_ref, received_ref):
    return jnp.where(info_ref[1] == 1, tokens_ref[info_ref[0]], received_ref[...])


def enter_kernel(info_ref, tokens_ref, received_ref, gain_ref, send_ref, normed_ref, outgoing_ref):
    stream = stream_of(info_ref, tokens_ref, received_ref).astype(F32)
    centred = stream - jnp.mean(stream, axis=-1, keepdims=True)
    variance = jnp.mean(centred * centred, axis=-1, keepdims=True)
    normed = (centred * lax.rsqrt(variance + 1e-05) * gain_ref[...]).astype(BF16)
    normed_ref[...] = normed
    outgoing_ref[...] = dot(send_ref[info_ref[0]], normed).astype(BF16)


def dense_kernel(
    parts,
    info_ref,
    tokens_ref,
    received_ref,
    normed_ref,
    picked_ref,
    router_ref,
    dense_in_ref,
    dense_out_ref,
    base_ref,
    gate_ref,
    in_ref,
    out_ref,
    sems,
):
    copies = fetches(dense_in_ref, dense_out_ref, in_ref, out_ref, sems, parts)
    for pair in copies:
        for copy in pair:
            copy.start()
    normed = normed_ref[...]
    logits = dot(normed, router_ref[...])
    labels = router_ref.shape[1]
    logit = jnp.sum(picked_ref[info_ref[0]][:, :labels] * logits, axis=1, keepdims=True)
    gate_ref[...] = jnp.broadcast_to(jax.nn.sigmoid(logit), gate_ref.shape)
    stream = stream_of(info_ref, tokens_ref, received_ref).astype(F32)
    base_ref[...] = stream + mlp(normed, in_ref, out_ref, copies)


def fetches(source_in, source_out, target_in, target_out, sems, parts):
    width = source_in.shape[1] // parts
    copies = []
    for part in range(parts):
        window = pl.ds(part * width, width)
        copies.append(
            (
                pltpu.make_async_copy(
                    source_in.at[:, window], target_in.at[:, window], sems.at[0, part]
                ),
                pltpu.make_async_copy(
                    source_out.at[window, :], target_out.at[window, :], sems.at[1, part]
                ),
            )
        )
    return copies


def mlp(token_rows, in_ref, out_ref, copies):
    width = in_ref.shape[1] // len(copies)
    total = None
    for part, (copy_in, copy_out) in enumerate(copies):
        window = pl.ds(part * width, width)
        copy_in.wait()
        activation = jax.nn.gelu(dot(token_rows, in_ref[:, window]), approximate=True).astype(BF16)
        copy_out.wait()
        product = dot(activation, out_ref[window, :])
        total = product if total is None else total + product
    return total


def expert_kernel(
    parts, info_ref, incoming_ref, expert_in_ref, expert_out_ref, result_ref, in_ref, out_ref, sems
):
    sources, rows, model_width = incoming_ref.shape
    half = rows // 2
    copies = [
        fetches(
            expert_in_ref.at[which],
            expert_out_ref.at[which],
            in_ref.at[which],
            out_ref.at[which],
            sems.at[which],
            parts,
        )
        for which in range(2)
    ]
    for pair in copies[0]:
        for copy in pair:
            copy.start()

    @pl.when(info_ref[2] == 1)
    def _():
        for pair in copies[1]:
            for copy in pair:
                copy.start()
        for which in range(2):
            window = pl.ds(which * half, half)
            token_rows = incoming_ref[:, window, :].reshape(sources * half, model_width)
            found = mlp(token_rows, in_ref.at[which], out_ref.at[which], copies[which])
            result_ref[:, window, :] = found.astype(BF16).reshape(sources, half, model_width)

    @pl.when(info_ref[2] == 0)
    def _():
        token_rows = incoming_ref[...].reshape(sources * rows, model_width)
        found = mlp(token_rows, in_ref.at[0], out_ref.at[0], copies[0])
        result_ref[...] = found.astype(BF16).reshape(sources, rows, model_width)


def leave_kernel(info_ref, base_ref, gate_ref, take_ref, returned_ref, stream_ref):
    routed = dot(take_ref[info_ref[0]], returned_ref[...])
    gate = gate_ref[:, :1]
    stream_ref[...] = (base_ref[...] + gate * routed).astype(BF16)


def split_kernel(first_ref, second_ref, out_ref):
    shares, tokens, share = out_ref.shape
    half = tokens // 2
    for number in range(shares):
        window = pl.ds(number * share, share)
        out_ref[number, :half, :] = first_ref[:, window]
        out_ref[number, half:, :] = second_ref[:, window]


def shape(dims, dtype):
    return jax.ShapeDtypeStruct(dims, dtype)


def body(tokens_in, ln_gain, router, dense_in, dense_out, expert_in, expert_out, routes):
    sections = lax.axis_size("section")
    members = lax.axis_size("expert")
    section_index = lax.axis_index("section")
    blocks, tok_dev, model_width = tokens_in.shape
    labels = router.shape[2]
    hidden_width = dense_in.shape[2]
    late = (section_index >= sections // 2).astype(jnp.int32)
    first = (section_index == 0).astype(jnp.int32)
    capacity = 2 * (tok_dev // labels)
    slots = labels * capacity
    params = pltpu.CompilerParams(vmem_limit_bytes=LIMIT)

    send, take, picked = pl.pallas_call(
        tables_kernel,
        out_shape=(
            shape((blocks, slots, tok_dev), BF16),
            shape((blocks, tok_dev, slots), BF16),
            shape((blocks, tok_dev, 128), F32),
        ),
        in_specs=[VMEM_SPEC],
        out_specs=[VMEM_SPEC] * 3,
        compiler_params=params,
    )(routes.reshape(blocks, tok_dev))

    def run(info, received):
        normed, outgoing = pl.pallas_call(
            enter_kernel,
            out_shape=(shape((tok_dev, model_width), BF16), shape((slots, model_width), BF16)),
            in_specs=[SMEM_SPEC] + [VMEM_SPEC] * 4,
            out_specs=[VMEM_SPEC] * 2,
            compiler_params=params,
        )(info, tokens_in, received, ln_gain, send)
        incoming = lax.all_to_all(
            outgoing.reshape(members, slots // members, model_width),
            "expert",
            split_axis=0,
            concat_axis=0,
            tiled=True,
        )
        base, gate = pl.pallas_call(
            functools.partial(dense_kernel, PARTS),
            out_shape=(shape((tok_dev, model_width), F32), shape((tok_dev, 128), F32)),
            in_specs=[SMEM_SPEC] + [VMEM_SPEC] * 5 + [HBM_SPEC] * 2,
            out_specs=[VMEM_SPEC] * 2,
            scratch_shapes=[
                pltpu.VMEM(dense_in.shape[1:], BF16),
                pltpu.VMEM(dense_out.shape[1:], BF16),
                pltpu.SemaphoreType.DMA((2, PARTS)),
            ],
            cost_estimate=pl.CostEstimate(
                flops=4 * tok_dev * model_width * hidden_width,
                transcendentals=tok_dev * hidden_width,
                bytes_accessed=8 << 20,
            ),
            compiler_params=params,
        )(info, tokens_in, received, normed, picked, router[0], dense_in[0], dense_out[0])
        results = pl.pallas_call(
            functools.partial(expert_kernel, PARTS),
            out_shape=shape(incoming.shape, BF16),
            in_specs=[SMEM_SPEC, VMEM_SPEC] + [HBM_SPEC] * 2,
            out_specs=VMEM_SPEC,
            scratch_shapes=[
                pltpu.VMEM(expert_in.shape[1:], BF16),
                pltpu.VMEM(expert_out.shape[1:], BF16),
                pltpu.SemaphoreType.DMA((2, 2, PARTS)),
            ],
            cost_estimate=pl.CostEstimate(
                flops=8 * tok_dev * model_width * hidden_width,
                transcendentals=2 * tok_dev * hidden_width,
                bytes_accessed=16 << 20,
            ),
            compiler_params=params,
        )(info, incoming, expert_in[0], expert_out[0])
        returned = lax.all_to_all(results, "expert", split_axis=0, concat_axis=0, tiled=True)
        return pl.pallas_call(
            leave_kernel,
            out_shape=shape((tok_dev, model_width), BF16),
            in_specs=[SMEM_SPEC] + [VMEM_SPEC] * 4,
            out_specs=VMEM_SPEC,
            compiler_params=params,
        )(info, base, gate, take, returned.reshape(slots, model_width))

    def step(number, carried):
        received, _, latest = carried
        block = number - section_index
        active = (block >= 0) & (block < blocks)
        info = jnp.stack([jnp.clip(block, 0, blocks - 1), first, late]).astype(jnp.int32)
        fresh = lax.cond(active, run, lambda info, received: received, info, received)
        received = lax.ppermute(
            fresh, "section", [(source, source + 1) for source in range(sections - 1)]
        )
        return received, latest, fresh

    nothing = jnp.zeros((tok_dev, model_width), BF16)
    _, before_last, last = lax.fori_loop(
        0, sections + blocks - 1, step, (nothing, nothing, nothing)
    )
    share = model_width // sections
    pieces = pl.pallas_call(
        split_kernel,
        out_shape=shape((sections, blocks * tok_dev, share), BF16),
        in_specs=[VMEM_SPEC] * 2,
        out_specs=VMEM_SPEC,
        compiler_params=params,
    )(before_last, last)
    spread = lax.all_to_all(pieces, "section", split_axis=0, concat_axis=0, tiled=True)
    return spread[sections - 1].reshape(blocks, tok_dev, share)


def solution(mesh):
    placed = (
        P(None, "expert", None),
        P("section", None),
        P("section", None, None),
        P("section", None, None),
        P("section", None, None),
        P("section", "expert", None, None),
        P("section", "expert", None, None),
        P("section", None, "expert", None),
    )
    return jax.shard_map(
        body, mesh=mesh, in_specs=placed, out_specs=P(None, "expert", "section"), check_vma=False
    )
```

time: 481 us -> 386 us (0.80)
  waiting for transfers between devices: 242 us -> 68 us
  blocking collectives: 0 us -> 137 us
  matrix products: 42.1 us -> 0 us
  Pallas kernels: 0 us -> 27.7 us
  local copies, waits for them, and re-layouts: 33.1 us -> 9.1 us
  between operations: 13.5 us -> 0.04 us
  other arithmetic: 9.63 us -> 0.72 us
  starting transfers between devices: 137 us -> 143 us
    all_to_all x18 -> x2, waiting for transfers between devices: 157 us -> 10 us  [run(): lax.all_to_all(results, 'expert', split_axis=0, concat_axis=0, tiled=True)]
    all_to_all x0 -> x3, blocking collectives: none -> 137 us  [the longest x1 111 us: body(): lax.all_to_all(pieces, 'section', split_axis=0, concat_axis=0, tiled=True)]
    ppermute x9, starting transfers between devices: 68.9 us -> 135 us  [step(): lax.ppermute(fresh, 'section', [(source, source + 1) for source in range(...]
    all_to_all x18 -> x2, starting transfers between devices: 68.3 us -> 7.17 us  [run(): lax.all_to_all(results, 'expert', split_axis=0, concat_axis=0, tiled=True)]
    all_gather x1 -> x0, waiting for transfers between devices: 49.6 us -> none  [picked_2(): lax.all_gather(value, axis)]
    dot_general x24 -> x0, matrix products: 42.1 us -> none  [the longest x4 20 us: expert_mlp(): jnp.dot(activation, weight_out, preferred_element_type=jnp.float32)]
    pallas_call x0 -> x10, Pallas kernels: none -> 27.7 us  [the longest x2 12.7 us: run(): pl.pallas_call(functools.partial(expert_kernel, PARTS), out_shape=shape(i...]
    ppermute x9, waiting for transfers between devices: 34.9 us -> 58 us  [step(): lax.ppermute(fresh, 'section', [(source, source + 1) for source in range(...]
  transfers between devices with their start and end apart: 28 -> 11, of which waited for: 28 -> 11; matrix products, arithmetic and copies ran while one was open for 3% -> 2% of each run, Pallas kernels for 0% -> 2%
where the time goes in v1:
time: 386 us; the launch traced here: 385 us
  starting transfers between devices  143 us (37%)
  blocking collectives  137 us (35%)
  waiting for transfers between devices  68 us (18%)
  Pallas kernels  27.7 us (7%)
  local copies, waits for them, and re-layouts  9.1 us (2%)
    ppermute x9, starting transfers between devices, step(): lax.ppermute(fresh, 'section', [(source, source + 1) for source in range(...  135 us
    all_to_all x1, blocking collectives, body(): lax.all_to_all(pieces, 'section', split_axis=0, concat_axis=0, tiled=True)  111 us
    ppermute x9, waiting for transfers between devices, step(): lax.ppermute(fresh, 'section', [(source, source + 1) for source in range(...  58 us
    all_to_all x2, blocking collectives, run(): lax.all_to_all(outgoing.reshape(members, slots // members, model_width),...  25.6 us
    pallas_call x2, Pallas kernels, run(): pl.pallas_call(functools.partial(expert_kernel, PARTS), out_shape=shape(i...  12.7 us
    all_to_all x2, waiting for transfers between devices, run(): lax.all_to_all(results, 'expert', split_axis=0, concat_axis=0, tiled=True)  10 us
    pallas_call x2, Pallas kernels, run(): pl.pallas_call(functools.partial(dense_kernel, PARTS), out_shape=(shape((...  8.98 us
  transfers between devices with their start and end apart: 11, of which 11 were waited for; matrix products, arithmetic and copies ran while one was open for 2% of the time, Pallas kernels for 2%

profile of v1, /device:TPU:1, one launch (start us, length us, event | category | flops | bytes accessed | tf_op | source)
XLA Modules:
  0.0 385.3 jit_solution(4506217191027990444)
XLA Ops:
  0.0 1.0 copy.9
  1.0 0.0 copy-start
  1.0 0.7 copy-done
  1.7 0.3 shard_map.82
  2.1 270.3 %while.20 = (s32[]{:T(128)}, bf16[128,1024]{1,0:T(8,128)(2,1)S(1)}, bf16[128,1024]{1,0:T(8,128)(2,1)}, bf16[128,1024]{1,0:T(8,128)(2,1)S(1)}, s32[]{:T(128)}, /*...) while((s32[]{:T(128)}, bf16[128,1024]{1,0:T(8,128)(2,1)S(1)}, ...), condition=%wide.region_3.4_spmd, body=%wide.region_0.3_spmd.sunk | while | flops 3221225472 | bytes 32506328 | solution.py:269
  2.1 0.1 pad_add_fusion.2
  2.2 4.9 %collective-permute-start = (bf16[128,1024]{1,0:T(8,128)(2,1)S(1)}, bf16[128,1024]{1,0:T(8,128)(2,1)S(1)}, u32[]{:S(2)}, u32[]{:S(2)}) collective-permute-start(bf16[128,1024]{1,0:T(8,128)(2,1)S(1)} %get-tuple-element.543), channel_id=1, source_target_pairs={{0,16},{16,32},{32,48},{48,64},{64,80},{80,96},{96,112},{1,17},{17... | collective-permute-start | bytes 786440 | tf_op jit(solution)/shard_map/while/body/eval_jaxpr/ppermute | solution.py:263
  7.1 0.7 copy.22
  7.9 37.5 %collective-permute-done = bf16[128,1024]{1,0:T(8,128)(2,1)S(1)} collective-permute-done((bf16[128,1024]{1,0:T(8,128)(2,1)S(1)}, bf16[128,1024]{1,0:T(8,128)(2,1)S(1)}, u32[]{:S(2)}, u32[]{:S(2)}) %collective-permute-start) | collective-permute-done | bytes 262176 | tf_op jit(solution)/shard_map/while/body/eval_jaxpr/ppermute | solution.py:263
  45.4 0.1 pad_add_fusion.2
  45.5 35.9 %conditional.2 = (bf16[128,1024]{1,0:T(8,128)(2,1)S(1)}) conditional(s32[]{:T(128)} %convert_element_type.16, bf16[128,1024]{1,0:T(8,128)(2,1)S(1)} %copy.17, (s32[3]{0:T(128)S(1)}, bf16[2,128,1024]{2,1,0:T(8,128)(2,1)}, bf16[128,1024]{1,0:T(8,128)(2,1)S(1)}, f32[1,1024]{1,0:T(1,128)}, bf16[2,256,128]{2,1,0:T(8,128)(2,1)S(1)}, ...), branch_computations={%region_1.1_spmd, %region_2.2_spmd} | conditional | flops 3221225472 | bytes 29884484 | solution.py:262
  45.5 1.6 branch_1_fun.4
  47.1 13.6 %all_to_all.13.incoming_ref = bf16[16,16,1024]{2,1,0:T(8,128)(2,1)S(1)} all-to-all(bf16[16,16,1024]{2,1,0:T(8,128)(2,1)S(1)} %bitcast.19), channel_id=1, replica_groups=mesh['section'=8,'expert'=16] {'expert'}, dimensions={0} | all-to-all | bytes 1048576 | tf_op jit(solution)/shard_map/while/body/eval_jaxpr/cond/branch_1_fun/all_to_all | solution.py:207
  60.6 0.0 copy-start.1
  60.6 6.3 %branch_1_fun.6 = bf16[16,16,1024]{2,1,0:T(8,128)(2,1)} custom-call(s32[3]{0:T(128)S(1)} %get-tuple-element.288.info_ref, bf16[16,16,1024]{2,1,0:T(8,128)(2,1)S(1)} %all_to_all.13.incoming_ref, bf16[2,1024,2048]{2,1,0:T(8,128)(2,1)} %bitcast.21, bf16[2,2048,1024]{2,1,0:T(8,128)(2,1)} %bitcast.22), custom_call_target="tpu_custom_call" | custom-call | flops 2147483648 | bytes 16777216 | tf_op jit(solution)/shard_map/while/body/eval_jaxpr/cond/branch_1_fun/pallas_call | solution.py:231
  67.0 3.6 all-to-all-start.1
  70.6 0.0 copy-done.1
  70.6 4.5 %branch_1_fun.5 = (f32[128,1024]{1,0:T(8,128)S(1)}, f32[128,128]{1,0:T(8,128)S(1)}) custom-call(s32[3]{0:T(128)S(1)} %get-tuple-element.288.info_ref, bf16[2,128,1024]{2,1,0:T(8,128)(2,1)S(1)} %copy-done.1, bf16[128,1024]{1,0:T(8,128)(2,1)S(1)} %get-tuple-element.290.received_ref, bf16[128,1024]{1,0:T(8,128)(2,1)S(1)} %get-tuple-element.293.normed_ref, ...), custom_call_target="tpu_custom_call" | custom-call | flops 1073741824 | bytes 8388608 | tf_op jit(solution)/shard_map/while/body/eval_jaxpr/cond/branch_1_fun/pallas_call | solution.py:214
  75.1 5.6 %all-to-all-done.1 = bf16[16,16,1024]{2,1,0:T(8,128)(2,1)S(1)} async-done(((bf16[16,16,1024]{2,1,0:T(8,128)(2,1)}), bf16[16,16,1024]{2,1,0:T(8,128)(2,1)S(1)}, u32[]{:S(2)}, u32[]{:S(2)}) %all-to-all-start.1) | async-done | bytes 524320 | tf_op jit(solution)/shard_map/while/body/eval_jaxpr/cond/branch_1_fun/all_to_all | solution.py:248
  80.6 0.8 branch_1_fun.7
  81.4 1.9 collective-permute-start
  83.4 0.7 copy.22
  84.1 2.6 collective-permute-done
  86.7 0.1 pad_add_fusion.2
  86.8 33.2 %conditional.2 = (bf16[128,1024]{1,0:T(8,128)(2,1)S(1)}) conditional(s32[]{:T(128)} %convert_element_type.16, bf16[128,1024]{1,0:T(8,128)(2,1)S(1)} %copy.17, (s32[3]{0:T(128)S(1)}, bf16[2,128,1024]{2,1,0:T(8,128)(2,1)}, bf16[128,1024]{1,0:T(8,128)(2,1)S(1)}, f32[1,1024]{1,0:T(1,128)}, bf16[2,256,128]{2,1,0:T(8,128)(2,1)S(1)}, ...), branch_computations={%region_1.1_spmd, %region_2.2_spmd} | conditional | flops 3221225472 | bytes 29884484 | solution.py:262
  86.8 1.6 branch_1_fun.4
  88.3 12.0 %all_to_all.13.incoming_ref = bf16[16,16,1024]{2,1,0:T(8,128)(2,1)S(1)} all-to-all(bf16[16,16,1024]{2,1,0:T(8,128)(2,1)S(1)} %bitcast.19), channel_id=1, replica_groups=mesh['section'=8,'expert'=16] {'expert'}, dimensions={0} | all-to-all | bytes 1048576 | tf_op jit(solution)/shard_map/while/body/eval_jaxpr/cond/branch_1_fun/all_to_all | solution.py:207
  100.3 0.0 copy-start.1
  100.3 6.3 %branch_1_fun.6 = bf16[16,16,1024]{2,1,0:T(8,128)(2,1)} custom-call(s32[3]{0:T(128)S(1)} %get-tuple-element.288.info_ref, bf16[16,16,1024]{2,1,0:T(8,128)(2,1)S(1)} %all_to_all.13.incoming_ref, bf16[2,1024,2048]{2,1,0:T(8,128)(2,1)} %bitcast.21, bf16[2,2048,1024]{2,1,0:T(8,128)(2,1)} %bitcast.22), custom_call_target="tpu_custom_call" | custom-call | flops 2147483648 | bytes 16777216 | tf_op jit(solution)/shard_map/while/body/eval_jaxpr/cond/branch_1_fun/pallas_call | solution.py:231
  106.7 3.6 all-to-all-start.1
  110.3 0.0 copy-done.1
  110.3 4.5 %branch_1_fun.5 = (f32[128,1024]{1,0:T(8,128)S(1)}, f32[128,128]{1,0:T(8,128)S(1)}) custom-call(s32[3]{0:T(128)S(1)} %get-tuple-element.288.info_ref, bf16[2,128,1024]{2,1,0:T(8,128)(2,1)S(1)} %copy-done.1, bf16[128,1024]{1,0:T(8,128)(2,1)S(1)} %get-tuple-element.290.received_ref, bf16[128,1024]{1,0:T(8,128)(2,1)S(1)} %get-tuple-element.293.normed_ref, ...), custom_call_target="tpu_custom_call" | custom-call | flops 1073741824 | bytes 8388608 | tf_op jit(solution)/shard_map/while/body/eval_jaxpr/cond/branch_1_fun/pallas_call | solution.py:214
  114.8 4.4 %all-to-all-done.1 = bf16[16,16,1024]{2,1,0:T(8,128)(2,1)S(1)} async-done(((bf16[16,16,1024]{2,1,0:T(8,128)(2,1)}), bf16[16,16,1024]{2,1,0:T(8,128)(2,1)S(1)}, u32[]{:S(2)}, u32[]{:S(2)}) %all-to-all-start.1) | async-done | bytes 524320 | tf_op jit(solution)/shard_map/while/body/eval_jaxpr/cond/branch_1_fun/all_to_all | solution.py:248
  119.2 0.8 branch_1_fun.7
  120.0 7.0 %collective-permute-start = (bf16[128,1024]{1,0:T(8,128)(2,1)S(1)}, bf16[128,1024]{1,0:T(8,128)(2,1)S(1)}, u32[]{:S(2)}, u32[]{:S(2)}) collective-permute-start(bf16[128,1024]{1,0:T(8,128)(2,1)S(1)} %get-tuple-element.543), channel_id=1, source_target_pairs={{0,16},{16,32},{32,48},{48,64},{64,80},{80,96},{96,112},{1,17},{17... | collective-permute-start | bytes 786440 | tf_op jit(solution)/shard_map/while/body/eval_jaxpr/ppermute | solution.py:263
  127.0 0.7 copy.22
  127.7 2.6 collective-permute-done
  130.3 0.1 pad_add_fusion.2
  130.4 39.9 %collective-permute-start = (bf16[128,1024]{1,0:T(8,128)(2,1)S(1)}, bf16[128,1024]{1,0:T(8,128)(2,1)S(1)}, u32[]{:S(2)}, u32[]{:S(2)}) collective-permute-start(bf16[128,1024]{1,0:T(8,128)(2,1)S(1)} %get-tuple-element.543), channel_id=1, source_target_pairs={{0,16},{16,32},{32,48},{48,64},{64,80},{80,96},{96,112},{1,17},{17... | collective-permute-start | bytes 786440 | tf_op jit(solution)/shard_map/while/body/eval_jaxpr/ppermute | solution.py:263
  170.2 0.7 copy.22
  171.0 2.6 collective-permute-done
  173.5 0.1 pad_add_fusion.2
  173.6 4.4 %collective-permute-start = (bf16[128,1024]{1,0:T(8,128)(2,1)S(1)}, bf16[128,1024]{1,0:T(8,128)(2,1)S(1)}, u32[]{:S(2)}, u32[]{:S(2)}) collective-permute-start(bf16[128,1024]{1,0:T(8,128)(2,1)S(1)} %get-tuple-element.543), channel_id=1, source_target_pairs={{0,16},{16,32},{32,48},{48,64},{64,80},{80,96},{96,112},{1,17},{17... | collective-permute-start | bytes 786440 | tf_op jit(solution)/shard_map/while/body/eval_jaxpr/ppermute | solution.py:263
  178.0 0.7 copy.22
  178.8 2.6 collective-permute-done
  181.3 0.1 pad_add_fusion.2
  181.4 28.4 %collective-permute-start = (bf16[128,1024]{1,0:T(8,128)(2,1)S(1)}, bf16[128,1024]{1,0:T(8,128)(2,1)S(1)}, u32[]{:S(2)}, u32[]{:S(2)}) collective-permute-start(bf16[128,1024]{1,0:T(8,128)(2,1)S(1)} %get-tuple-element.543), channel_id=1, source_target_pairs={{0,16},{16,32},{32,48},{48,64},{64,80},{80,96},{96,112},{1,17},{17... | collective-permute-start | bytes 786440 | tf_op jit(solution)/shard_map/while/body/eval_jaxpr/ppermute | solution.py:263
  209.8 0.7 copy.22
  210.6 2.6 collective-permute-done
  213.1 0.1 pad_add_fusion.2
  213.2 4.4 %collective-permute-start = (bf16[128,1024]{1,0:T(8,128)(2,1)S(1)}, bf16[128,1024]{1,0:T(8,128)(2,1)S(1)}, u32[]{:S(2)}, u32[]{:S(2)}) collective-permute-start(bf16[128,1024]{1,0:T(8,128)(2,1)S(1)} %get-tuple-element.543), channel_id=1, source_target_pairs={{0,16},{16,32},{32,48},{48,64},{64,80},{80,96},{96,112},{1,17},{17... | collective-permute-start | bytes 786440 | tf_op jit(solution)/shard_map/while/body/eval_jaxpr/ppermute | solution.py:263
  217.6 0.7 copy.22
  218.3 2.6 collective-permute-done
  220.9 0.1 pad_add_fusion.2
  221.0 40.3 %collective-permute-start = (bf16[128,1024]{1,0:T(8,128)(2,1)S(1)}, bf16[128,1024]{1,0:T(8,128)(2,1)S(1)}, u32[]{:S(2)}, u32[]{:S(2)}) collective-permute-start(bf16[128,1024]{1,0:T(8,128)(2,1)S(1)} %get-tuple-element.543), channel_id=1, source_target_pairs={{0,16},{16,32},{32,48},{48,64},{64,80},{80,96},{96,112},{1,17},{17... | collective-permute-start | bytes 786440 | tf_op jit(solution)/shard_map/while/body/eval_jaxpr/ppermute | solution.py:263
  261.3 0.7 copy.22
  262.0 2.6 collective-permute-done
  264.6 0.1 pad_add_fusion.2
  264.7 4.4 %collective-permute-start = (bf16[128,1024]{1,0:T(8,128)(2,1)S(1)}, bf16[128,1024]{1,0:T(8,128)(2,1)S(1)}, u32[]{:S(2)}, u32[]{:S(2)}) collective-permute-start(bf16[128,1024]{1,0:T(8,128)(2,1)S(1)} %get-tuple-element.543), channel_id=1, source_target_pairs={{0,16},{16,32},{32,48},{48,64},{64,80},{80,96},{96,112},{1,17},{17... | collective-permute-start | bytes 786440 | tf_op jit(solution)/shard_map/while/body/eval_jaxpr/ppermute | solution.py:263
  269.1 0.7 copy.22
  269.8 2.6 collective-permute-done
  272.4 1.0 shard_map.83
  273.4 111.2 %all_to_all.14 = bf16[8,256,128]{2,1,0:T(8,128)(2,1)S(1)} all-to-all(bf16[8,256,128]{2,1,0:T(8,128)(2,1)S(1)} %shard_map.83), channel_id=1, replica_groups=mesh['section'=8,'expert'=16] {'section'}, dimensions={0} | all-to-all | bytes 1048576 | tf_op jit(solution)/shard_map/all_to_all | solution.py:280
  384.6 0.6 slice.4
  (28 shorter events, 0.4 us)
Async XLA Ops:
  1.0 0.7 copy-start
  2.2 43.2 %collective-permute-start = (bf16[128,1024]{1,0:T(8,128)(2,1)S(1)}, bf16[128,1024]{1,0:T(8,128)(2,1)S(1)}, u32[]{:S(2)}, u32[]{:S(2)}) collective-permute-start(bf16[128,1024]{1,0:T(8,128)(2,1)S(1)} %get-tuple-element.543), channel_id=1, source_target_pairs={{0,16},{16,32},{32,48},{48,64},{64,80},{80,96},{96,112},{1,17},{17... | collective-permute-start | bytes 786440 | tf_op jit(solution)/shard_map/while/body/eval_jaxpr/ppermute | solution.py:263
  60.6 9.9 %copy-start.1 = (bf16[2,128,1024]{2,1,0:T(8,128)(2,1)S(1)}, bf16[2,128,1024]{2,1,0:T(8,128)(2,1)}, u32[]{:S(2)}) copy-start(bf16[2,128,1024]{2,1,0:T(8,128)(2,1)} %get-tuple-element.289.tokens_ref) | copy-start | bytes 1572868 | tf_op jit(solution)/shard_map/while/body/eval_jaxpr/cond
  67.0 13.7 %all-to-all-start.1 = ((bf16[16,16,1024]{2,1,0:T(8,128)(2,1)}), bf16[16,16,1024]{2,1,0:T(8,128)(2,1)S(1)}, u32[]{:S(2)}, u32[]{:S(2)}) async-start(bf16[16,16,1024]{2,1,0:T(8,128)(2,1)} %branch_1_fun.6), calls=%async_computation.1 | async-start | bytes 1048576 | tf_op jit(solution)/shard_map/while/body/eval_jaxpr/cond/branch_1_fun/all_to_all | solution.py:248
  81.4 5.2 %collective-permute-start = (bf16[128,1024]{1,0:T(8,128)(2,1)S(1)}, bf16[128,1024]{1,0:T(8,128)(2,1)S(1)}, u32[]{:S(2)}, u32[]{:S(2)}) collective-permute-start(bf16[128,1024]{1,0:T(8,128)(2,1)S(1)} %get-tuple-element.543), channel_id=1, source_target_pairs={{0,16},{16,32},{32,48},{48,64},{64,80},{80,96},{96,112},{1,17},{17... | collective-permute-start | bytes 786440 | tf_op jit(solution)/shard_map/while/body/eval_jaxpr/ppermute | solution.py:263
  100.3 9.9 %copy-start.1 = (bf16[2,128,1024]{2,1,0:T(8,128)(2,1)S(1)}, bf16[2,128,1024]{2,1,0:T(8,128)(2,1)}, u32[]{:S(2)}) copy-start(bf16[2,128,1024]{2,1,0:T(8,128)(2,1)} %get-tuple-element.289.tokens_ref) | copy-start | bytes 1572868 | tf_op jit(solution)/shard_map/while/body/eval_jaxpr/cond
  106.7 12.5 %all-to-all-start.1 = ((bf16[16,16,1024]{2,1,0:T(8,128)(2,1)}), bf16[16,16,1024]{2,1,0:T(8,128)(2,1)S(1)}, u32[]{:S(2)}, u32[]{:S(2)}) async-start(bf16[16,16,1024]{2,1,0:T(8,128)(2,1)} %branch_1_fun.6), calls=%async_computation.1 | async-start | bytes 1048576 | tf_op jit(solution)/shard_map/while/body/eval_jaxpr/cond/branch_1_fun/all_to_all | solution.py:248
  120.0 10.3 %collective-permute-start = (bf16[128,1024]{1,0:T(8,128)(2,1)S(1)}, bf16[128,1024]{1,0:T(8,128)(2,1)S(1)}, u32[]{:S(2)}, u32[]{:S(2)}) collective-permute-start(bf16[128,1024]{1,0:T(8,128)(2,1)S(1)} %get-tuple-element.543), channel_id=1, source_target_pairs={{0,16},{16,32},{32,48},{48,64},{64,80},{80,96},{96,112},{1,17},{17... | collective-permute-start | bytes 786440 | tf_op jit(solution)/shard_map/while/body/eval_jaxpr/ppermute | solution.py:263
  130.4 43.2 %collective-permute-start = (bf16[128,1024]{1,0:T(8,128)(2,1)S(1)}, bf16[128,1024]{1,0:T(8,128)(2,1)S(1)}, u32[]{:S(2)}, u32[]{:S(2)}) collective-permute-start(bf16[128,1024]{1,0:T(8,128)(2,1)S(1)} %get-tuple-element.543), channel_id=1, source_target_pairs={{0,16},{16,32},{32,48},{48,64},{64,80},{80,96},{96,112},{1,17},{17... | collective-permute-start | bytes 786440 | tf_op jit(solution)/shard_map/while/body/eval_jaxpr/ppermute | solution.py:263
  173.6 7.7 %collective-permute-start = (bf16[128,1024]{1,0:T(8,128)(2,1)S(1)}, bf16[128,1024]{1,0:T(8,128)(2,1)S(1)}, u32[]{:S(2)}, u32[]{:S(2)}) collective-permute-start(bf16[128,1024]{1,0:T(8,128)(2,1)S(1)} %get-tuple-element.543), channel_id=1, source_target_pairs={{0,16},{16,32},{32,48},{48,64},{64,80},{80,96},{96,112},{1,17},{17... | collective-permute-start | bytes 786440 | tf_op jit(solution)/shard_map/while/body/eval_jaxpr/ppermute | solution.py:263
  181.4 31.7 %collective-permute-start = (bf16[128,1024]{1,0:T(8,128)(2,1)S(1)}, bf16[128,1024]{1,0:T(8,128)(2,1)S(1)}, u32[]{:S(2)}, u32[]{:S(2)}) collective-permute-start(bf16[128,1024]{1,0:T(8,128)(2,1)S(1)} %get-tuple-element.543), channel_id=1, source_target_pairs={{0,16},{16,32},{32,48},{48,64},{64,80},{80,96},{96,112},{1,17},{17... | collective-permute-start | bytes 786440 | tf_op jit(solution)/shard_map/while/body/eval_jaxpr/ppermute | solution.py:263
  213.2 7.7 %collective-permute-start = (bf16[128,1024]{1,0:T(8,128)(2,1)S(1)}, bf16[128,1024]{1,0:T(8,128)(2,1)S(1)}, u32[]{:S(2)}, u32[]{:S(2)}) collective-permute-start(bf16[128,1024]{1,0:T(8,128)(2,1)S(1)} %get-tuple-element.543), channel_id=1, source_target_pairs={{0,16},{16,32},{32,48},{48,64},{64,80},{80,96},{96,112},{1,17},{17... | collective-permute-start | bytes 786440 | tf_op jit(solution)/shard_map/while/body/eval_jaxpr/ppermute | solution.py:263
  221.0 43.6 %collective-permute-start = (bf16[128,1024]{1,0:T(8,128)(2,1)S(1)}, bf16[128,1024]{1,0:T(8,128)(2,1)S(1)}, u32[]{:S(2)}, u32[]{:S(2)}) collective-permute-start(bf16[128,1024]{1,0:T(8,128)(2,1)S(1)} %get-tuple-element.543), channel_id=1, source_target_pairs={{0,16},{16,32},{32,48},{48,64},{64,80},{80,96},{96,112},{1,17},{17... | collective-permute-start | bytes 786440 | tf_op jit(solution)/shard_map/while/body/eval_jaxpr/ppermute | solution.py:263
  264.7 7.7 %collective-permute-start = (bf16[128,1024]{1,0:T(8,128)(2,1)S(1)}, bf16[128,1024]{1,0:T(8,128)(2,1)S(1)}, u32[]{:S(2)}, u32[]{:S(2)}) collective-permute-start(bf16[128,1024]{1,0:T(8,128)(2,1)S(1)} %get-tuple-element.543), channel_id=1, source_target_pairs={{0,16},{16,32},{32,48},{48,64},{64,80},{80,96},{96,112},{1,17},{17... | collective-permute-start | bytes 786440 | tf_op jit(solution)/shard_map/while/body/eval_jaxpr/ppermute | solution.py:263

commit v2 on v1

--- a/solution.py
+++ b/solution.py
@@ -41,12 +41,8 @@
         picked_ref[block] = picked.T
 
 
-def stream_of(info_ref, tokens_ref, received_ref):
-    return jnp.where(info_ref[1] == 1, tokens_ref[info_ref[0]], received_ref[...])
-
-
-def enter_kernel(info_ref, tokens_ref, received_ref, gain_ref, send_ref, normed_ref, outgoing_ref):
-    stream = stream_of(info_ref, tokens_ref, received_ref).astype(F32)
+def enter_kernel(info_ref, received_ref, gain_ref, send_ref, normed_ref, outgoing_ref):
+    stream = received_ref[...].astype(F32)
     centred = stream - jnp.mean(stream, axis=-1, keepdims=True)
     variance = jnp.mean(centred * centred, axis=-1, keepdims=True)
     normed = (centred * lax.rsqrt(variance + 1e-05) * gain_ref[...]).astype(BF16)
@@ -57,7 +53,6 @@
 def dense_kernel(
     parts,
     info_ref,
-    tokens_ref,
     received_ref,
     normed_ref,
     picked_ref,
@@ -70,7 +65,20 @@
     out_ref,
     sems,
 ):
-    copies = fetches(dense_in_ref, dense_out_ref, in_ref, out_ref, sems, parts)
+    width = in_ref.shape[1] // parts
+    copies = []
+    for part in range(parts):
+        window = pl.ds(part * width, width)
+        copies.append(
+            (
+                pltpu.make_async_copy(
+                    dense_in_ref.at[:, window], in_ref.at[:, window], sems.at[0, part]
+                ),
+                pltpu.make_async_copy(
+                    dense_out_ref.at[window, :], out_ref.at[window, :], sems.at[1, part]
+                ),
+            )
+        )
     for pair in copies:
         for copy in pair:
             copy.start()
@@ -79,77 +87,40 @@
     labels = router_ref.shape[1]
     logit = jnp.sum(picked_ref[info_ref[0]][:, :labels] * logits, axis=1, keepdims=True)
     gate_ref[...] = jnp.broadcast_to(jax.nn.sigmoid(logit), gate_ref.shape)
-    stream = stream_of(info_ref, tokens_ref, received_ref).astype(F32)
-    base_ref[...] = stream + mlp(normed, in_ref, out_ref, copies)
-
-
-def fetches(source_in, source_out, target_in, target_out, sems, parts):
-    width = source_in.shape[1] // parts
-    copies = []
-    for part in range(parts):
-        window = pl.ds(part * width, width)
-        copies.append(
-            (
-                pltpu.make_async_copy(
-                    source_in.at[:, window], target_in.at[:, window], sems.at[0, part]
-                ),
-                pltpu.make_async_copy(
-                    source_out.at[window, :], target_out.at[window, :], sems.at[1, part]
-                ),
-            )
-        )
-    return copies
-
-
-def mlp(token_rows, in_ref, out_ref, copies):
-    width = in_ref.shape[1] // len(copies)
-    total = None
+    total = received_ref[...].astype(F32)
+    dense_part = None
     for part, (copy_in, copy_out) in enumerate(copies):
         window = pl.ds(part * width, width)
         copy_in.wait()
-        activation = jax.nn.gelu(dot(token_rows, in_ref[:, window]), approximate=True).astype(BF16)
+        hidden = jax.nn.gelu(dot(normed, in_ref[:, window]), approximate=True).astype(BF16)
         copy_out.wait()
-        product = dot(activation, out_ref[window, :])
-        total = product if total is None else total + product
-    return total
-
-
-def expert_kernel(
-    parts, info_ref, incoming_ref, expert_in_ref, expert_out_ref, result_ref, in_ref, out_ref, sems
-):
+        product = dot(hidden, out_ref[window, :])
+        dense_part = product if dense_part is None else dense_part + product
+    base_ref[...] = total + dense_part
+
+
+def mlp(token_rows, weight_in, weight_out):
+    activation = jax.nn.gelu(dot(token_rows, weight_in), approximate=True).astype(BF16)
+    return dot(activation, weight_out).astype(BF16)
+
+
+def expert_kernel(info_ref, incoming_ref, expert_in_ref, expert_out_ref, result_ref):
     sources, rows, model_width = incoming_ref.shape
     half = rows // 2
-    copies = [
-        fetches(
-            expert_in_ref.at[which],
-            expert_out_ref.at[which],
-            in_ref.at[which],
-            out_ref.at[which],
-            sems.at[which],
-            parts,
-        )
-        for which in range(2)
-    ]
-    for pair in copies[0]:
-        for copy in pair:
-            copy.start()
-
-    @pl.when(info_ref[2] == 1)
+
+    @pl.when(info_ref[1] == 1)
     def _():
-        for pair in copies[1]:
-            for copy in pair:
-                copy.start()
         for which in range(2):
             window = pl.ds(which * half, half)
             token_rows = incoming_ref[:, window, :].reshape(sources * half, model_width)
-            found = mlp(token_rows, in_ref.at[which], out_ref.at[which], copies[which])
-            result_ref[:, window, :] = found.astype(BF16).reshape(sources, half, model_width)
-
-    @pl.when(info_ref[2] == 0)
+            found = mlp(token_rows, expert_in_ref[which], expert_out_ref[which])
+            result_ref[:, window, :] = found.reshape(sources, half, model_width)
+
+    @pl.when(info_ref[1] == 0)
     def _():
         token_rows = incoming_ref[...].reshape(sources * rows, model_width)
-        found = mlp(token_rows, in_ref.at[0], out_ref.at[0], copies[0])
-        result_ref[...] = found.astype(BF16).reshape(sources, rows, model_width)
+        found = mlp(token_rows, expert_in_ref[0], expert_out_ref[0])
+        result_ref[...] = found.reshape(sources, rows, model_width)
 
 
 def leave_kernel(info_ref, base_ref, gate_ref, take_ref, returned_ref, stream_ref):
@@ -179,7 +150,6 @@
     labels = router.shape[2]
     hidden_width = dense_in.shape[2]
     late = (section_index >= sections // 2).astype(jnp.int32)
-    first = (section_index == 0).astype(jnp.int32)
     capacity = 2 * (tok_dev // labels)
     slots = labels * capacity
     params = pltpu.CompilerParams(vmem_limit_bytes=LIMIT)
@@ -200,10 +170,13 @@
         normed, outgoing = pl.pallas_call(
             enter_kernel,
             out_shape=(shape((tok_dev, model_width), BF16), shape((slots, model_width), BF16)),
-            in_specs=[SMEM_SPEC] + [VMEM_SPEC] * 4,
+            in_specs=[SMEM_SPEC] + [VMEM_SPEC] * 3,
             out_specs=[VMEM_SPEC] * 2,
-            compiler_params=params,
-        )(info, tokens_in, received, ln_gain, send)
+            cost_estimate=pl.CostEstimate(
+                flops=20_000_000_000, transcendentals=0, bytes_accessed=40 << 20
+            ),
+            compiler_params=params,
+        )(info, received, ln_gain, send)
         incoming = lax.all_to_all(
             outgoing.reshape(members, slots // members, model_width),
             "expert",
@@ -214,7 +187,7 @@
         base, gate = pl.pallas_call(
             functools.partial(dense_kernel, PARTS),
             out_shape=(shape((tok_dev, model_width), F32), shape((tok_dev, 128), F32)),
-            in_specs=[SMEM_SPEC] + [VMEM_SPEC] * 5 + [HBM_SPEC] * 2,
+            in_specs=[SMEM_SPEC] + [VMEM_SPEC] * 4 + [HBM_SPEC] * 2,
             out_specs=[VMEM_SPEC] * 2,
             scratch_shapes=[
                 pltpu.VMEM(dense_in.shape[1:], BF16),
@@ -227,17 +200,12 @@
                 bytes_accessed=8 << 20,
             ),
             compiler_params=params,
-        )(info, tokens_in, received, normed, picked, router[0], dense_in[0], dense_out[0])
+        )(info, received, normed, picked, router[0], dense_in[0], dense_out[0])
         results = pl.pallas_call(
-            functools.partial(expert_kernel, PARTS),
+            expert_kernel,
             out_shape=shape(incoming.shape, BF16),
-            in_specs=[SMEM_SPEC, VMEM_SPEC] + [HBM_SPEC] * 2,
+            in_specs=[SMEM_SPEC] + [VMEM_SPEC] * 3,
             out_specs=VMEM_SPEC,
-            scratch_shapes=[
-                pltpu.VMEM(expert_in.shape[1:], BF16),
-                pltpu.VMEM(expert_out.shape[1:], BF16),
-                pltpu.SemaphoreType.DMA((2, 2, PARTS)),
-            ],
             cost_estimate=pl.CostEstimate(
                 flops=8 * tok_dev * model_width * hidden_width,
                 transcendentals=2 * tok_dev * hidden_width,
@@ -258,16 +226,15 @@
         received, _, latest = carried
         block = number - section_index
         active = (block >= 0) & (block < blocks)
-        info = jnp.stack([jnp.clip(block, 0, blocks - 1), first, late]).astype(jnp.int32)
-        fresh = lax.cond(active, run, lambda info, received: received, info, received)
+        info = jnp.stack([jnp.clip(block, 0, blocks - 1), late]).astype(jnp.int32)
+        fresh = lax.cond(active, run, lambda info, received: tokens_in[blocks - 1], info, received)
         received = lax.ppermute(
-            fresh, "section", [(source, source + 1) for source in range(sections - 1)]
+            fresh, "section", [(source, (source + 1) % sections) for source in range(sections)]
         )
         return received, latest, fresh
 
-    nothing = jnp.zeros((tok_dev, model_width), BF16)
     _, before_last, last = lax.fori_loop(
-        0, sections + blocks - 1, step, (nothing, nothing, nothing)
+        0, sections + blocks - 1, step, (tokens_in[0], tokens_in[0], tokens_in[0])
     )
     share = model_width // sections
     pieces = pl.pallas_call(

time: 386 us -> 345 us (0.89)
  blocking collectives: 137 us -> 74 us
  waiting for transfers between devices: 68 us -> 122 us
  starting transfers between devices: 143 us -> 108 us
  local copies, waits for them, and re-layouts: 9.1 us -> 17.3 us
  Pallas kernels: 27.7 us -> 22.4 us
    all_to_all x1, blocking collectives: 111 us -> 49.8 us  [body(): lax.all_to_all(pieces, 'section', split_axis=0, concat_axis=0, tiled=True)]
    ppermute x9, waiting for transfers between devices: 58 us -> 113 us  [step(): lax.ppermute(fresh, 'section', [(source, (source + 1) % sections) for sou...]
    ppermute x9, starting transfers between devices: 135 us -> 101 us  [step(): lax.ppermute(fresh, 'section', [(source, (source + 1) % sections) for sou...]
    squeeze x0 -> x8, local copies, waits for them, and re-layouts: none -> 7.74 us  [the longest x7 6.77 us: step(): tokens_in[blocks - 1]]
    pallas_call x2, Pallas kernels: 12.7 us -> 7.76 us  [run(): pl.pallas_call(expert_kernel, out_shape=shape(incoming.shape, BF16), in_s...]
  transfers between devices with their start and end apart: 11 -> 11, of which waited for: 11 -> 11; matrix products, arithmetic and copies ran while one was open for 2% -> 2% of each run, Pallas kernels for 2% -> 3%
where the time goes in v2:
time: 345 us; the launch traced here: 344 us
  waiting for transfers between devices  122 us (35%)
  starting transfers between devices  108 us (31%)
  blocking collectives  74 us (21%)
  Pallas kernels  22.4 us (6%)
  local copies, waits for them, and re-layouts  17.3 us (5%)
    ppermute x9, waiting for transfers between devices, step(): lax.ppermute(fresh, 'section', [(source, (source + 1) % sections) for sou...  113 us
    ppermute x9, starting transfers between devices, step(): lax.ppermute(fresh, 'section', [(source, (source + 1) % sections) for sou...  101 us
    all_to_all x1, blocking collectives, body(): lax.all_to_all(pieces, 'section', split_axis=0, concat_axis=0, tiled=True)  49.8 us
    all_to_all x2, blocking collectives, run(): lax.all_to_all(outgoing.reshape(members, slots // members, model_width),...  24.3 us
    pallas_call x2, Pallas kernels, run(): pl.pallas_call(functools.partial(dense_kernel, PARTS), out_shape=(shape((...  9.05 us
    all_to_all x2, waiting for transfers between devices, run(): lax.all_to_all(results, 'expert', split_axis=0, concat_axis=0, tiled=True)  8.84 us
    pallas_call x2, Pallas kernels, run(): pl.pallas_call(expert_kernel, out_shape=shape(incoming.shape, BF16), in_s...  7.76 us
    all_to_all x2, starting transfers between devices, run(): lax.all_to_all(results, 'expert', split_axis=0, concat_axis=0, tiled=True)  7.14 us
  transfers between devices with their start and end apart: 11, of which 11 were waited for; matrix products, arithmetic and copies ran while one was open for 2% of the time, Pallas kernels for 3%

profile of v2, /device:TPU:1, one launch (start us, length us, event | category | flops | bytes accessed | tf_op | source)
XLA Modules:
  0.0 343.9 jit_solution(18183662149352270091)
XLA Ops:
  0.0 1.0 slice_bitcast_fusion.1
  1.0 0.7 copy.14
  1.7 1.0 copy.9
  2.7 0.7 copy-done
  3.4 0.3 shard_map.85
  3.7 288.8 %while.17 = (s32[]{:T(128)}, bf16[128,1024]{1,0:T(8,128)(2,1)S(1)}, bf16[128,1024]{1,0:T(8,128)(2,1)}, bf16[128,1024]{1,0:T(8,128)(2,1)S(1)}, s32[]{:T(128)}, /*...) while((s32[]{:T(128)}, bf16[128,1024]{1,0:T(8,128)(2,1)S(1)}, ...), condition=%wide.region_3.4_spmd, body=%wide.region_0.3_spmd.sunk | while | flops 23221225472 | bytes 138936816 | solution.py:236
  3.8 1.0 conditional.2
  3.8 1.0 slice_bitcast_fusion
  4.8 3.0 collective-permute-start
  7.8 0.7 copy.22
  8.6 34.7 %collective-permute-done = bf16[128,1024]{1,0:T(8,128)(2,1)S(1)} collective-permute-done((bf16[128,1024]{1,0:T(8,128)(2,1)S(1)}, bf16[128,1024]{1,0:T(8,128)(2,1)S(1)}, u32[]{:S(2)}, u32[]{:S(2)}) %collective-permute-start) | collective-permute-done | bytes 262176 | tf_op jit(solution)/shard_map/while/body/eval_jaxpr/ppermute | solution.py:231
  43.4 30.7 %conditional.2 = (bf16[128,1024]{1,0:T(8,128)(2,1)S(1)}) conditional(s32[]{:T(128)} %convert_element_type.12, bf16[2,128,1024]{2,1,0:T(8,128)(2,1)} %get-tuple-element.500, (s32[2]{0:T(128)S(1)}, bf16[128,1024]{1,0:T(8,128)(2,1)S(1)}, f32[1,1024]{1,0:T(1,128)}, bf16[2,256,128]{2,1,0:T(8,128)(2,1)S(1)}, bf16[1,1024,32]{2,1,0:T(8,128)(2,1)S(1)}, ...), branch_computations={%region_1.1_spmd, %region_2.2_spmd} | conditional | flops 23221225472 | bytes 136839264 | solution.py:230
  43.4 1.4 branch_1_fun.4
  44.8 12.1 %all_to_all.13.incoming_ref = bf16[16,16,1024]{2,1,0:T(8,128)(2,1)S(1)} all-to-all(bf16[16,16,1024]{2,1,0:T(8,128)(2,1)S(1)} %bitcast.20), channel_id=1, replica_groups=mesh['section'=8,'expert'=16] {'expert'}, dimensions={0} | all-to-all | bytes 1048576 | tf_op jit(solution)/shard_map/while/body/eval_jaxpr/cond/branch_1_fun/all_to_all | solution.py:180
  56.9 3.9 %branch_1_fun.6 = bf16[16,16,1024]{2,1,0:T(8,128)(2,1)} custom-call(s32[2]{0:T(128)S(1)} %get-tuple-element.272.info_ref, bf16[16,16,1024]{2,1,0:T(8,128)(2,1)S(1)} %all_to_all.13.incoming_ref, bf16[2,1024,2048]{2,1,0:T(8,128)(2,1)S(1)} %bitcast.22, bf16[2,2048,1024]{2,1,0:T(8,128)(2,1)S(1)} %bitcast.23), custom_call_target="tpu_custom_call" | custom-call | flops 2147483648 | bytes 16777216 | tf_op jit(solution)/shard_map/while/body/eval_jaxpr/cond/branch_1_fun/pallas_call | solution.py:204
  60.8 3.6 %all-to-all-start.1 = ((bf16[16,16,1024]{2,1,0:T(8,128)(2,1)}), bf16[16,16,1024]{2,1,0:T(8,128)(2,1)S(1)}, u32[]{:S(2)}, u32[]{:S(2)}) async-start(bf16[16,16,1024]{2,1,0:T(8,128)(2,1)} %branch_1_fun.6), calls=%async_computation.1 | async-start | bytes 1048576 | tf_op jit(solution)/shard_map/while/body/eval_jaxpr/cond/branch_1_fun/all_to_all | solution.py:216
  64.4 4.5 %branch_1_fun.5 = (f32[128,1024]{1,0:T(8,128)S(1)}, f32[128,128]{1,0:T(8,128)S(1)}) custom-call(s32[2]{0:T(128)S(1)} %get-tuple-element.272.info_ref, bf16[128,1024]{1,0:T(8,128)(2,1)S(1)} %get-tuple-element.273.received_ref, bf16[128,1024]{1,0:T(8,128)(2,1)S(1)} %get-tuple-element.276.normed_ref, f32[2,128,128]{2,1,0:T(8,128)S(1)} %get-tuple-element.277.picked_ref, ...), custom_call_target="tpu_custom_call" | custom-call | flops 1073741824 | bytes 8388608 | tf_op jit(solution)/shard_map/while/body/eval_jaxpr/cond/branch_1_fun/pallas_call | solution.py:187
  68.9 4.4 %all-to-all-done.1 = bf16[16,16,1024]{2,1,0:T(8,128)(2,1)S(1)} async-done(((bf16[16,16,1024]{2,1,0:T(8,128)(2,1)}), bf16[16,16,1024]{2,1,0:T(8,128)(2,1)S(1)}, u32[]{:S(2)}, u32[]{:S(2)}) %all-to-all-start.1) | async-done | bytes 524320 | tf_op jit(solution)/shard_map/while/body/eval_jaxpr/cond/branch_1_fun/all_to_all | solution.py:216
  73.3 0.8 branch_1_fun.7
  74.1 0.7 copy.22
  74.8 8.6 %collective-permute-done = bf16[128,1024]{1,0:T(8,128)(2,1)S(1)} collective-permute-done((bf16[128,1024]{1,0:T(8,128)(2,1)S(1)}, bf16[128,1024]{1,0:T(8,128)(2,1)S(1)}, u32[]{:S(2)}, u32[]{:S(2)}) %collective-permute-start) | collective-permute-done | bytes 262176 | tf_op jit(solution)/shard_map/while/body/eval_jaxpr/ppermute | solution.py:231
  83.5 30.7 %conditional.2 = (bf16[128,1024]{1,0:T(8,128)(2,1)S(1)}) conditional(s32[]{:T(128)} %convert_element_type.12, bf16[2,128,1024]{2,1,0:T(8,128)(2,1)} %get-tuple-element.500, (s32[2]{0:T(128)S(1)}, bf16[128,1024]{1,0:T(8,128)(2,1)S(1)}, f32[1,1024]{1,0:T(1,128)}, bf16[2,256,128]{2,1,0:T(8,128)(2,1)S(1)}, bf16[1,1024,32]{2,1,0:T(8,128)(2,1)S(1)}, ...), branch_computations={%region_1.1_spmd, %region_2.2_spmd} | conditional | flops 23221225472 | bytes 136839264 | solution.py:230
  83.5 1.4 branch_1_fun.4
  84.9 12.1 %all_to_all.13.incoming_ref = bf16[16,16,1024]{2,1,0:T(8,128)(2,1)S(1)} all-to-all(bf16[16,16,1024]{2,1,0:T(8,128)(2,1)S(1)} %bitcast.20), channel_id=1, replica_groups=mesh['section'=8,'expert'=16] {'expert'}, dimensions={0} | all-to-all | bytes 1048576 | tf_op jit(solution)/shard_map/while/body/eval_jaxpr/cond/branch_1_fun/all_to_all | solution.py:180
  97.1 3.9 %branch_1_fun.6 = bf16[16,16,1024]{2,1,0:T(8,128)(2,1)} custom-call(s32[2]{0:T(128)S(1)} %get-tuple-element.272.info_ref, bf16[16,16,1024]{2,1,0:T(8,128)(2,1)S(1)} %all_to_all.13.incoming_ref, bf16[2,1024,2048]{2,1,0:T(8,128)(2,1)S(1)} %bitcast.22, bf16[2,2048,1024]{2,1,0:T(8,128)(2,1)S(1)} %bitcast.23), custom_call_target="tpu_custom_call" | custom-call | flops 2147483648 | bytes 16777216 | tf_op jit(solution)/shard_map/while/body/eval_jaxpr/cond/branch_1_fun/pallas_call | solution.py:204
  100.9 3.6 %all-to-all-start.1 = ((bf16[16,16,1024]{2,1,0:T(8,128)(2,1)}), bf16[16,16,1024]{2,1,0:T(8,128)(2,1)S(1)}, u32[]{:S(2)}, u32[]{:S(2)}) async-start(bf16[16,16,1024]{2,1,0:T(8,128)(2,1)} %branch_1_fun.6), calls=%async_computation.1 | async-start | bytes 1048576 | tf_op jit(solution)/shard_map/while/body/eval_jaxpr/cond/branch_1_fun/all_to_all | solution.py:216
  104.5 4.5 %branch_1_fun.5 = (f32[128,1024]{1,0:T(8,128)S(1)}, f32[128,128]{1,0:T(8,128)S(1)}) custom-call(s32[2]{0:T(128)S(1)} %get-tuple-element.272.info_ref, bf16[128,1024]{1,0:T(8,128)(2,1)S(1)} %get-tuple-element.273.received_ref, bf16[128,1024]{1,0:T(8,128)(2,1)S(1)} %get-tuple-element.276.normed_ref, f32[2,128,128]{2,1,0:T(8,128)S(1)} %get-tuple-element.277.picked_ref, ...), custom_call_target="tpu_custom_call" | custom-call | flops 1073741824 | bytes 8388608 | tf_op jit(solution)/shard_map/while/body/eval_jaxpr/cond/branch_1_fun/pallas_call | solution.py:187
  109.0 4.4 %all-to-all-done.1 = bf16[16,16,1024]{2,1,0:T(8,128)(2,1)S(1)} async-done(((bf16[16,16,1024]{2,1,0:T(8,128)(2,1)}), bf16[16,16,1024]{2,1,0:T(8,128)(2,1)S(1)}, u32[]{:S(2)}, u32[]{:S(2)}) %all-to-all-start.1) | async-done | bytes 524320 | tf_op jit(solution)/shard_map/while/body/eval_jaxpr/cond/branch_1_fun/all_to_all | solution.py:216
  113.5 0.8 branch_1_fun.7
  114.3 0.7 copy.22
  115.0 2.6 collective-permute-done
  117.7 1.0 conditional.2
  117.7 1.0 slice_bitcast_fusion
  118.6 34.6 %collective-permute-start = (bf16[128,1024]{1,0:T(8,128)(2,1)S(1)}, bf16[128,1024]{1,0:T(8,128)(2,1)S(1)}, u32[]{:S(2)}, u32[]{:S(2)}) collective-permute-start(bf16[128,1024]{1,0:T(8,128)(2,1)S(1)} %get-tuple-element.513), channel_id=1, source_target_pairs={{0,16},{16,32},{32,48},{48,64},{64,80},{80,96},{96,112},{112,0},{1... | collective-permute-start | bytes 786440 | tf_op jit(solution)/shard_map/while/body/eval_jaxpr/ppermute | solution.py:231
  153.2 0.7 copy.22
  153.9 2.6 collective-permute-done
  156.6 1.0 conditional.2
  156.6 1.0 slice_bitcast_fusion
  157.6 2.5 collective-permute-start
  160.1 0.7 copy.22
  160.8 2.6 collective-permute-done
  163.5 1.0 conditional.2
  163.5 1.0 slice_bitcast_fusion
  164.4 23.3 %collective-permute-start = (bf16[128,1024]{1,0:T(8,128)(2,1)S(1)}, bf16[128,1024]{1,0:T(8,128)(2,1)S(1)}, u32[]{:S(2)}, u32[]{:S(2)}) collective-permute-start(bf16[128,1024]{1,0:T(8,128)(2,1)S(1)} %get-tuple-element.513), channel_id=1, source_target_pairs={{0,16},{16,32},{32,48},{48,64},{64,80},{80,96},{96,112},{112,0},{1... | collective-permute-start | bytes 786440 | tf_op jit(solution)/shard_map/while/body/eval_jaxpr/ppermute | solution.py:231
  187.8 0.7 copy.22
  188.5 2.6 collective-permute-done
  191.2 1.0 conditional.2
  191.2 1.0 slice_bitcast_fusion
  192.1 2.5 collective-permute-start
  194.6 0.7 copy.22
  195.4 2.6 collective-permute-done
  198.0 1.0 conditional.2
  198.0 1.0 slice_bitcast_fusion
  199.0 32.1 %collective-permute-start = (bf16[128,1024]{1,0:T(8,128)(2,1)S(1)}, bf16[128,1024]{1,0:T(8,128)(2,1)S(1)}, u32[]{:S(2)}, u32[]{:S(2)}) collective-permute-start(bf16[128,1024]{1,0:T(8,128)(2,1)S(1)} %get-tuple-element.513), channel_id=1, source_target_pairs={{0,16},{16,32},{32,48},{48,64},{64,80},{80,96},{96,112},{112,0},{1... | collective-permute-start | bytes 786440 | tf_op jit(solution)/shard_map/while/body/eval_jaxpr/ppermute | solution.py:231
  231.1 0.7 copy.22
  231.8 2.6 collective-permute-done
  234.5 1.0 conditional.2
  234.5 1.0 slice_bitcast_fusion
  235.5 2.5 collective-permute-start
  238.0 0.7 copy.22
  238.7 53.8 %collective-permute-done = bf16[128,1024]{1,0:T(8,128)(2,1)S(1)} collective-permute-done((bf16[128,1024]{1,0:T(8,128)(2,1)S(1)}, bf16[128,1024]{1,0:T(8,128)(2,1)S(1)}, u32[]{:S(2)}, u32[]{:S(2)}) %collective-permute-start) | collective-permute-done | bytes 262176 | tf_op jit(solution)/shard_map/while/body/eval_jaxpr/ppermute | solution.py:231
  292.5 1.0 shard_map.86
  293.5 49.8 %all_to_all.14 = bf16[8,256,128]{2,1,0:T(8,128)(2,1)S(1)} all-to-all(bf16[8,256,128]{2,1,0:T(8,128)(2,1)S(1)} %shard_map.86), channel_id=1, replica_groups=mesh['section'=8,'expert'=16] {'section'}, dimensions={0} | all-to-all | bytes 1048576 | tf_op jit(solution)/shard_map/all_to_all | solution.py:247
  343.3 0.6 slice.13
  (30 shorter events, 0.9 us)
Async XLA Ops:
  2.7 0.7 copy-start
  4.8 38.5 %collective-permute-start = (bf16[128,1024]{1,0:T(8,128)(2,1)S(1)}, bf16[128,1024]{1,0:T(8,128)(2,1)S(1)}, u32[]{:S(2)}, u32[]{:S(2)}) collective-permute-start(bf16[128,1024]{1,0:T(8,128)(2,1)S(1)} %get-tuple-element.513), channel_id=1, source_target_pairs={{0,16},{16,32},{32,48},{48,64},{64,80},{80,96},{96,112},{112,0},{1... | collective-permute-start | bytes 786440 | tf_op jit(solution)/shard_map/while/body/eval_jaxpr/ppermute | solution.py:231
  43.4 13.5 %copy-start.1 = (bf16[1,2,1024,2048]{3,2,1,0:T(8,128)(2,1)S(1)}, bf16[1,2,1024,2048]{3,2,1,0:T(8,128)(2,1)}, u32[]{:S(2)}) copy-start(bf16[1,2,1024,2048]{3,2,1,0:T(8,128)(2,1)} %get-tuple-element.285) | copy-start | bytes 25165828 | tf_op jit(solution)/shard_map/while/body/eval_jaxpr/cond
  43.4 13.5 %copy-start.2 = (bf16[1,2,2048,1024]{3,2,1,0:T(8,128)(2,1)S(1)}, bf16[1,2,2048,1024]{3,2,1,0:T(8,128)(2,1)}, u32[]{:S(2)}) copy-start(bf16[1,2,2048,1024]{3,2,1,0:T(8,128)(2,1)} %get-tuple-element.286) | copy-start | bytes 25165828 | tf_op jit(solution)/shard_map/while/body/eval_jaxpr/cond
  60.8 12.5 %all-to-all-start.1 = ((bf16[16,16,1024]{2,1,0:T(8,128)(2,1)}), bf16[16,16,1024]{2,1,0:T(8,128)(2,1)S(1)}, u32[]{:S(2)}, u32[]{:S(2)}) async-start(bf16[16,16,1024]{2,1,0:T(8,128)(2,1)} %branch_1_fun.6), calls=%async_computation.1 | async-start | bytes 1048576 | tf_op jit(solution)/shard_map/while/body/eval_jaxpr/cond/branch_1_fun/all_to_all | solution.py:216
  74.1 9.4 %collective-permute-start = (bf16[128,1024]{1,0:T(8,128)(2,1)S(1)}, bf16[128,1024]{1,0:T(8,128)(2,1)S(1)}, u32[]{:S(2)}, u32[]{:S(2)}) collective-permute-start(bf16[128,1024]{1,0:T(8,128)(2,1)S(1)} %get-tuple-element.513), channel_id=1, source_target_pairs={{0,16},{16,32},{32,48},{48,64},{64,80},{80,96},{96,112},{112,0},{1... | collective-permute-start | bytes 786440 | tf_op jit(solution)/shard_map/while/body/eval_jaxpr/ppermute | solution.py:231
  83.5 13.5 %copy-start.1 = (bf16[1,2,1024,2048]{3,2,1,0:T(8,128)(2,1)S(1)}, bf16[1,2,1024,2048]{3,2,1,0:T(8,128)(2,1)}, u32[]{:S(2)}) copy-start(bf16[1,2,1024,2048]{3,2,1,0:T(8,128)(2,1)} %get-tuple-element.285) | copy-start | bytes 25165828 | tf_op jit(solution)/shard_map/while/body/eval_jaxpr/cond
  83.5 13.5 %copy-start.2 = (bf16[1,2,2048,1024]{3,2,1,0:T(8,128)(2,1)S(1)}, bf16[1,2,2048,1024]{3,2,1,0:T(8,128)(2,1)}, u32[]{:S(2)}) copy-start(bf16[1,2,2048,1024]{3,2,1,0:T(8,128)(2,1)} %get-tuple-element.286) | copy-start | bytes 25165828 | tf_op jit(solution)/shard_map/while/body/eval_jaxpr/cond
  100.9 12.5 %all-to-all-start.1 = ((bf16[16,16,1024]{2,1,0:T(8,128)(2,1)}), bf16[16,16,1024]{2,1,0:T(8,128)(2,1)S(1)}, u32[]{:S(2)}, u32[]{:S(2)}) async-start(bf16[16,16,1024]{2,1,0:T(8,128)(2,1)} %branch_1_fun.6), calls=%async_computation.1 | async-start | bytes 1048576 | tf_op jit(solution)/shard_map/while/body/eval_jaxpr/cond/branch_1_fun/all_to_all | solution.py:216
  114.2 3.3 collective-permute-start
  118.6 37.9 %collective-permute-start = (bf16[128,1024]{1,0:T(8,128)(2,1)S(1)}, bf16[128,1024]{1,0:T(8,128)(2,1)S(1)}, u32[]{:S(2)}, u32[]{:S(2)}) collective-permute-start(bf16[128,1024]{1,0:T(8,128)(2,1)S(1)} %get-tuple-element.513), channel_id=1, source_target_pairs={{0,16},{16,32},{32,48},{48,64},{64,80},{80,96},{96,112},{112,0},{1... | collective-permute-start | bytes 786440 | tf_op jit(solution)/shard_map/while/body/eval_jaxpr/ppermute | solution.py:231
  157.6 5.8 %collective-permute-start = (bf16[128,1024]{1,0:T(8,128)(2,1)S(1)}, bf16[128,1024]{1,0:T(8,128)(2,1)S(1)}, u32[]{:S(2)}, u32[]{:S(2)}) collective-permute-start(bf16[128,1024]{1,0:T(8,128)(2,1)S(1)} %get-tuple-element.513), channel_id=1, source_target_pairs={{0,16},{16,32},{32,48},{48,64},{64,80},{80,96},{96,112},{112,0},{1... | collective-permute-start | bytes 786440 | tf_op jit(solution)/shard_map/while/body/eval_jaxpr/ppermute | solution.py:231
  164.4 26.6 %collective-permute-start = (bf16[128,1024]{1,0:T(8,128)(2,1)S(1)}, bf16[128,1024]{1,0:T(8,128)(2,1)S(1)}, u32[]{:S(2)}, u32[]{:S(2)}) collective-permute-start(bf16[128,1024]{1,0:T(8,128)(2,1)S(1)} %get-tuple-element.513), channel_id=1, source_target_pairs={{0,16},{16,32},{32,48},{48,64},{64,80},{80,96},{96,112},{112,0},{1... | collective-permute-start | bytes 786440 | tf_op jit(solution)/shard_map/while/body/eval_jaxpr/ppermute | solution.py:231
  192.1 5.8 %collective-permute-start = (bf16[128,1024]{1,0:T(8,128)(2,1)S(1)}, bf16[128,1024]{1,0:T(8,128)(2,1)S(1)}, u32[]{:S(2)}, u32[]{:S(2)}) collective-permute-start(bf16[128,1024]{1,0:T(8,128)(2,1)S(1)} %get-tuple-element.513), channel_id=1, source_target_pairs={{0,16},{16,32},{32,48},{48,64},{64,80},{80,96},{96,112},{112,0},{1... | collective-permute-start | bytes 786440 | tf_op jit(solution)/shard_map/while/body/eval_jaxpr/ppermute | solution.py:231
  199.0 35.4 %collective-permute-start = (bf16[128,1024]{1,0:T(8,128)(2,1)S(1)}, bf16[128,1024]{1,0:T(8,128)(2,1)S(1)}, u32[]{:S(2)}, u32[]{:S(2)}) collective-permute-start(bf16[128,1024]{1,0:T(8,128)(2,1)S(1)} %get-tuple-element.513), channel_id=1, source_target_pairs={{0,16},{16,32},{32,48},{48,64},{64,80},{80,96},{96,112},{112,0},{1... | collective-permute-start | bytes 786440 | tf_op jit(solution)/shard_map/while/body/eval_jaxpr/ppermute | solution.py:231
  235.5 57.0 %collective-permute-start = (bf16[128,1024]{1,0:T(8,128)(2,1)S(1)}, bf16[128,1024]{1,0:T(8,128)(2,1)S(1)}, u32[]{:S(2)}, u32[]{:S(2)}) collective-permute-start(bf16[128,1024]{1,0:T(8,128)(2,1)S(1)} %get-tuple-element.513), channel_id=1, source_target_pairs={{0,16},{16,32},{32,48},{48,64},{64,80},{80,96},{96,112},{112,0},{1... | collective-permute-start | bytes 786440 | tf_op jit(solution)/shard_map/while/body/eval_jaxpr/ppermute | solution.py:231
